TPU v7x, 32 devices: a whole 2x2x4 slice. The times are simulated.
32 devices in a mesh: dp: 16 (over z, y, x), tensor: 2 (over core).
Axes of the slice: x: 2, y: 2, z: 4, core: 2. Of those that a mesh axis runs over, the one named last changes fastest.
Arguments:
- tokens: bfloat16 [25088, 1024], P('dp'), may hold values from -6 to 6
- attention_gain: float32 [1024], replicated, may hold values from 0.25 to 1.75
- attention_shift: float32 [1024], replicated, may hold values from -3 to 3
- input_weight: bfloat16 [1024, 3, 1024], P(None, None, 'tensor'), may hold values from -0.1875 to 0.1875
- query_bias: float32 [1024], P('tensor'), may hold values from -3 to 3
- value_bias: float32 [1024], P('tensor'), may hold values from -3 to 3
- output_weight: bfloat16 [1024, 1024], P('tensor'), may hold values from -1.5 to 1.5
- output_bias: float32 [1024], replicated, may hold values from -3 to 3
- feedforward_gain: float32 [1024], replicated, may hold values from 0.25 to 1.75
- feedforward_shift: float32 [1024], replicated, may hold values from -3 to 3
- expand_weight: bfloat16 [1024, 4096], P(None, 'tensor'), may hold values from -0.1875 to 0.1875
- expand_bias: float32 [4096], P('tensor'), may hold values from -3 to 3
- reduce_weight: bfloat16 [4096, 1024], P('tensor'), may hold values from -0.09375 to 0.09375
- reduce_bias: float32 [1024], replicated, may hold values from -3 to 3
- cotangent: bfloat16 [25088, 1024], P('dp'), may hold values from -6 to 6
Outputs:
- block_out: bfloat16 [25088, 1024], P('dp')
- tokens_gradient: bfloat16 [25088, 1024], P('dp')
- attention_gain_gradient: float32 [1024], replicated
- attention_shift_gradient: float32 [1024], replicated
- input_weight_gradient: float32 [1024, 3, 1024], P(None, None, 'tensor')
- query_bias_gradient: float32 [1024], P('tensor')
- value_bias_gradient: float32 [1024], P('tensor')
- output_weight_gradient: float32 [1024, 1024], P('tensor')
- output_bias_gradient: float32 [1024], replicated
- feedforward_gain_gradient: float32 [1024], replicated
- feedforward_shift_gradient: float32 [1024], replicated
- expand_weight_gradient: float32 [1024, 4096], P(None, 'tensor')
- expand_bias_gradient: float32 [4096], P('tensor')
- reduce_weight_gradient: float32 [4096, 1024], P('tensor')
- reduce_bias_gradient: float32 [1024], replicated
All inputs are finite; a program needn't handle non-finite values.
Results may differ from a plain program's by a relative error of at most 0.013.
The roundings to bfloat16 on the way count: a program that leaves them out, or rounds other values in their place, can miss the bound.
Values may be sent and summed in bfloat16 or wider, within the bound.
A program may use at most 384 MiB of HBM per device.

v0:
```python
import functools

import jax
import jax.numpy as jnp
from jax import lax
from jax.experimental import pallas as pl
from jax.experimental.pallas import tpu as pltpu
from jax.sharding import PartitionSpec as P


HEAD_DIM = 64
PAIR = 2 * HEAD_DIM
F32 = jnp.float32
BF16 = jnp.bfloat16
EXP_SCALE = 0.125 * 1.4426950408889634


norm_eps = 1e-06


def layer_norm(values, gain, shift):
    center = values - jnp.mean(values, axis=-1, keepdims=True)
    spread = jnp.mean(center * center, axis=-1, keepdims=True)
    return center * lax.rsqrt(spread + norm_eps) * gain + shift


def dot_nn(a, b):
    return lax.dot_general(a, b, (((1,), (0,)), ((), ())), preferred_element_type=F32)


def dot_nt(a, b):
    return lax.dot_general(a, b, (((1,), (1,)), ((), ())), preferred_element_type=F32)


def dot_tn(a, b):
    return lax.dot_general(a, b, (((0,), (0,)), ((), ())), preferred_element_type=F32)


def attend_kernel(q_ref, k_ref, v_ref, out_ref, exact_ref, inverse_ref, weights_ref):
    low_half = lax.broadcasted_iota(jnp.int32, (1, PAIR), 1) < HEAD_DIM
    zero = jnp.zeros((), BF16)
    keys, values, queries = k_ref[...], v_ref[...], q_ref[...]
    mixed, inverses = [], []
    for head in range(2):
        own_keys = jnp.where(low_half if head == 0 else ~low_half, keys, zero)
        scores = dot_nt(queries, own_keys)
        top = jnp.max(scores, axis=1, keepdims=True)
        weights = jnp.exp2((scores - top) * EXP_SCALE)
        inverse = 1.0 / jnp.sum(weights, axis=1, keepdims=True)
        weights = weights.astype(BF16)
        weights_ref[head] = weights
        mixed.append(dot_nn(weights, values) * inverse)
        inverses.append(inverse)
    exact = jnp.where(low_half, mixed[0], mixed[1])
    out_ref[...] = exact.astype(BF16)
    exact_ref[...] = exact
    inverse_ref[...] = jnp.where(low_half, inverses[0], inverses[1])


def attend(queries, keys, values, block=224):
    rows, width = queries.shape
    pairs = width // PAIR
    tile = pl.BlockSpec((block, PAIR), lambda p, i: (i, p))
    whole = pl.BlockSpec((rows, PAIR), lambda p, i: (0, p))
    return pl.pallas_call(
        attend_kernel,
        grid=(pairs, rows // block),
        in_specs=[tile, whole, whole],
        out_specs=[tile, tile, tile, pl.BlockSpec((2, block, rows), lambda p, i: (p, i, 0))],
        out_shape=[
            jax.ShapeDtypeStruct((rows, width), BF16),
            jax.ShapeDtypeStruct((rows, width), F32),
            jax.ShapeDtypeStruct((rows, width), F32),
            jax.ShapeDtypeStruct((2 * pairs, rows, rows), BF16),
        ],
        compiler_params=pltpu.CompilerParams(vmem_limit_bytes=60 << 20),
        cost_estimate=pl.CostEstimate(
            flops=8 * pairs * rows * rows * HEAD_DIM * 4,
            bytes_accessed=4 * pairs * rows * rows,
            transcendentals=2 * pairs * rows * rows,
        ),
        name="attend",
    )(queries, keys, values)


def feed_kernel(n_ref, c_ref, expand_ref, reduce_ref, bias_ref, act_ref, grad_ref, sum_ref, *, chunk):
    @pl.when(pl.program_id(0) == 0)
    def _():
        sum_ref[...] = jnp.zeros_like(sum_ref)

    normed, cotangent = n_ref[...], c_ref[...]
    for first in range(0, expand_ref.shape[1], chunk):
        cols = pl.ds(first, chunk)
        hidden = dot_nn(normed, expand_ref[:, cols]) + bias_ref[:, cols]
        pushed = dot_nt(cotangent, reduce_ref[cols, :])
        share = 0.5 * lax.erf(hidden * ROOT_HALF) + 0.5
        act_ref[:, cols] = (hidden * share).astype(BF16)
        density = jnp.exp2(hidden * hidden * HALF_LOG2E) * NORMAL_PEAK
        grad = (pushed * (share + hidden * density)).astype(BF16)
        grad_ref[:, cols] = grad
        sum_ref[:, cols] += jnp.sum(grad.astype(F32), axis=0, keepdims=True)


def feed(normed, cotangent, expand_weight, reduce_weight, expand_bias, block=224, chunk=256):
    rows, depth = normed.shape
    width = expand_weight.shape[1]
    tile = pl.BlockSpec((block, depth), lambda i: (i, 0))
    out = pl.BlockSpec((block, width), lambda i: (i, 0))

    def whole(shape):
        return pl.BlockSpec(shape, lambda i: (0, 0))

    act, grad, total = pl.pallas_call(
        functools.partial(feed_kernel, chunk=chunk),
        grid=(rows // block,),
        in_specs=[tile, tile, whole((depth, width)), whole((width, depth)), whole((1, width))],
        out_specs=[out, out, whole((1, width))],
        out_shape=[jax.ShapeDtypeStruct((rows, width), BF16)] * 2 + [jax.ShapeDtypeStruct((1, width), F32)],
        compiler_params=pltpu.CompilerParams(vmem_limit_bytes=60 << 20),
        cost_estimate=pl.CostEstimate(
            flops=4 * rows * depth * width, bytes_accessed=8 * rows * (depth + width), transcendentals=rows * width
        ),
        name="feed",
    )(normed, cotangent, expand_weight, reduce_weight, expand_bias.reshape(1, -1))
    return act, grad, total.reshape(-1)


def orders_of(bits):
    if bits == 4:
        return ((0, 1, 2, 3), (1, 0, 2, 3), (2, 0, 1, 3), (2, 1, 0, 3))
    return tuple(tuple((i + j) % bits for j in range(bits)) for i in (0, 1, 2, 3))


class Part:
    def __init__(self, array, first, each, cols, dtype, order, outer):
        self.array, self.first, self.each = array, first, each
        self.cols, self.dtype, self.order, self.outer = cols, dtype, order, outer
        self.inner = order[1:] if outer else order
        self.depth = len(self.inner)
        self.shards = 1 << self.depth
        self.half_rows = self.shards * each


def parts_of(array, shape, dtype, n, shares, orders, outer=True):
    unit = 16 if dtype == BF16 else 8
    units = shape[0] // (n * unit)
    counts = [units * share // sum(shares) for share in shares]
    counts[0] += units - sum(counts)
    parts, first = [], 0
    for count, order in zip(counts, orders):
        if count:
            parts.append(Part(array, first, count * unit, shape[1], dtype, order, outer))
            first += n * count * unit
    return parts


def divides(shape, dtype, n):
    return shape[0] % (n * (16 if dtype == BF16 else 8)) == 0


FEED_PARTS = (
    ((2, 2, 2, 2), ((1, 2, 0, 3), (2, 0, 3, 1), (0, 3, 2, 1), (1, 0, 3, 2))),
    ((2, 1, 1), ((0, 1, 2, 3), (1, 0, 2, 3), (3, 1, 0, 2))),
)
FEED_STEPS = ((2, 0), (5, 0), (0, 0), (1, 0), (5, 1), (4, 0), (3, 0), (1, 1), (2, 1), (6, 0), (3, 1), (4, 1), (5, 2), (2, 2), (1, 2), (0, 1), (0, 2), (1, 3), (5, 3), (6, 1), (3, 2), (4, 2), (6, 2), (3, 3), (1, 4), (6, 3), (0, 3), (6, 4), (4, 3), (2, 3), (2, 4), (3, 4), (1, 5), (4, 4), (6, 5), (0, 4), (5, 4), (2, 5), (0, 5), (3, 5), (4, 5), (5, 5), (3, 6), (6, 6), (1, 6), (4, 6), (5, 6), (0, 6), (2, 6))
FEED_SLOTS = (0, 0, 0, 0, 3, 3, 4, 6, 6, 6, 8, 9, 9, 9, 9, 10, 11, 13, 14, 14, 14, 15, 16, 17, 17, 19, 19, 21, 21, 21, 22, 22, 23, 25, 25, 25, 25, 25, 27, 28, 29, 30, 31, 31, 31, 34, 34, 35, 35)
REST_PARTS = (
    ((2, 2, 4, 2, 2), ((1, 0, 3, 2), (2, 3, 1, 0), (0, 1, 2, 3), (1, 0, 3, 2), (2, 1, 0, 3))),
    ((1, 1), ((0, 2, 1, 3), (1, 0, 3, 2))),
)
REST_STEPS = ((1, 0), (2, 0), (0, 0), (3, 0), (5, 0), (0, 1), (3, 1), (1, 1), (5, 1), (2, 1), (6, 0), (4, 0), (6, 1), (1, 2), (0, 2), (2, 2), (0, 3), (6, 2), (5, 2), (3, 2), (4, 1), (0, 4), (3, 3), (4, 2), (2, 3), (6, 3), (4, 3), (5, 3), (1, 3), (3, 4), (1, 4), (2, 4), (4, 4), (0, 5), (6, 4), (1, 5), (5, 4), (4, 5), (3, 5), (0, 6), (2, 5), (5, 5), (6, 5), (4, 6), (2, 6), (6, 6), (3, 6), (5, 6), (1, 6))


def feed_plan(shapes, n):
    if n == 16:
        parts = [parts_of(i, s, BF16, n, *FEED_PARTS[i]) for i, s in enumerate(shapes)]
        if sum(len(p) for p in parts) == 7:
            return sum(parts, []), FEED_STEPS, FEED_SLOTS
    orders = orders_of(n.bit_length() - 1)
    parts = sum((parts_of(i, s, BF16, n, (1, 1), orders[2 * i : 2 * i + 2]) for i, s in enumerate(shapes)), [])
    steps = [(i, s) for s in range(2 * parts[0].depth + 1) for i in range(len(parts))]
    return parts, steps, None


def rest_plan(shapes, n):
    if n == 16:
        parts = [parts_of(i, s, BF16, n, *REST_PARTS[i]) for i, s in enumerate(shapes)]
        if sum(len(p) for p in parts) == 7:
            return sum(parts, []), REST_STEPS
    orders = orders_of(n.bit_length() - 1)
    parts = sum((parts_of(i, s, BF16, n, (1,), orders[i : i + 1]) for i, s in enumerate(shapes)), [])
    return parts, [(i, s) for s in range(2 * parts[0].depth + 1) for i in range(len(parts))]


def swap_bit(values, bit, n):
    return lax.ppermute(values, "dp", [(j, j ^ (1 << bit)) for j in range(n)])


def bit_of_index(bit):
    return (lax.axis_index("dp") >> bit) & 1


def outer_gift(array, part):
    other = 1 - bit_of_index(part.order[0])
    return lax.dynamic_slice_in_dim(array, part.first + other * part.half_rows, part.half_rows, 0)


def join_kernel(parts, *refs):
    count = len(parts)
    halves, outs = refs[: 2 * count], refs[2 * count : -2 - 4 * count]
    takes, gives = refs[-2 - 4 * count : -2 - 2 * count], refs[-2 - 2 * count : -2]
    take_sem, give_sem = refs[-2:]
    copies = []
    for k in range(2 * count):
        pltpu.make_async_copy(halves[k], takes[k], take_sem.at[k]).start()
    me = lax.axis_index("dp")
    for k in range(2 * count):
        part = parts[k // 2]
        digit = (me // (1 << part.order[0])) % 2
        place = digit if k % 2 == 0 else 1 - digit
        pltpu.make_async_copy(halves[k], takes[k], take_sem.at[k]).wait()
        gives[k][...] = takes[k][...].astype(F32)
        rows = pl.ds(pl.multiple_of(part.first + place * part.half_rows, 8), part.half_rows)
        copies.append(pltpu.make_async_copy(gives[k], outs[part.array].at[rows, :], give_sem.at[k]))
        copies[-1].start()
    for copy in copies:
        copy.wait()


def join(parts, owns, others, shapes):
    halves = [half for pair in zip(owns, others) for half in pair]
    anywhere = pl.BlockSpec(memory_space=pl.ANY)
    takes = [pltpu.VMEM(half.shape, half.dtype) for half in halves]
    gives = [pltpu.VMEM(half.shape, F32) for half in halves]
    size = sum(shape[0] * shape[1] for shape in shapes)
    return pl.pallas_call(
        functools.partial(join_kernel, parts),
        in_specs=[anywhere] * len(halves),
        out_specs=[anywhere] * len(shapes),
        out_shape=[jax.ShapeDtypeStruct(shape, F32) for shape in shapes],
        scratch_shapes=takes
        + gives
        + [pltpu.SemaphoreType.DMA((len(halves),))] * 2,
        compiler_params=pltpu.CompilerParams(vmem_limit_bytes=60 << 20),
        cost_estimate=pl.CostEstimate(flops=size, bytes_accessed=6 * size, transcendentals=0),
        name="join",
    )(*halves)


class Reduction:
    def __init__(self, parts, bits, bufs, lands, gathers, sems):
        self.parts, self.bits = parts, bits
        self.bufs, self.lands, self.gathers = bufs, lands, gathers
        self.load_sem, self.store_sem, self.send_sem, self.recv_sem = sems
        me = lax.axis_index("dp")
        self.digit = [(me // (1 << b)) % 2 for b in range(bits)]
        self.partner = [me + (1 << b) * (1 - 2 * self.digit[b]) for b in range(bits)]

    def greet(self):
        barrier = pltpu.get_barrier_semaphore()
        for b in range(self.bits):
            pl.semaphore_signal(
                barrier, inc=1, device_id={"dp": self.partner[b]}, device_id_type=pl.DeviceIdType.MESH
            )
        pl.semaphore_wait(barrier, self.bits)

    def rows(self, i, position, base=0):
        part, shard = self.parts[i], 0
        for level, b in enumerate(part.inner):
            flip = (position >> (part.depth - 1 - level)) & 1
            shard = shard + (1 << (part.depth - 1 - level)) * ((1 - self.digit[b]) if flip else self.digit[b])
        return pl.ds(pl.multiple_of(base + shard * part.each, 8), part.each)

    def load(self, i, ref, recv):
        part = self.parts[i]
        base = part.first + (self.digit[part.order[0]] * part.half_rows if part.outer else 0)
        for position in range(part.shards):
            pltpu.make_async_copy(
                ref.at[self.rows(i, position, base), :], self.bufs[i].at[position], self.load_sem.at[2 * i]
            ).start()
            if part.outer:
                pltpu.make_async_copy(
                    recv.at[self.rows(i, position), :], self.lands[i].at[position], self.load_sem.at[2 * i + 1]
                ).start()

    def begin(self, i):
        part, buf, land = self.parts[i], self.bufs[i], self.lands[i]
        pltpu.make_async_copy(buf, buf, self.load_sem.at[2 * i]).wait()
        if part.outer:
            got = land.at[pl.ds(0, part.shards)]
            pltpu.make_async_copy(got, got, self.load_sem.at[2 * i + 1]).wait()
            self.add(i, 0, part.shards, buf)

    def add(self, i, start, count, to):
        buf, land = self.bufs[i], self.lands[i]

        def body(j, carry):
            to[j] = (buf[j].astype(F32) + land[start + j].astype(F32)).astype(buf.dtype)
            return carry

        lax.fori_loop(0, count, body, 0)

    def store(self, i, ref):
        base = 0 if self.parts[i].outer else self.parts[i].first
        for position in range(self.parts[i].shards):
            pltpu.make_async_copy(
                self.gathers[i].at[position], ref.at[self.rows(i, position, base), :], self.store_sem.at[i]
            ).start()

    def store_wait(self, i):
        pltpu.make_async_copy(self.gathers[i], self.gathers[i], self.store_sem.at[i]).wait()

    def exchange(self, i, number):
        part = self.parts[i]
        level = number if number < part.depth else 2 * part.depth - 1 - number
        half = part.shards >> (level + 1)
        if number < part.depth:
            at = (part.shards if part.outer else 0) + part.shards - 2 * half
            source, target = self.bufs[i].at[pl.ds(half, half)], self.lands[i].at[pl.ds(at, half)]
        else:
            source, target = self.gathers[i].at[pl.ds(0, half)], self.gathers[i].at[pl.ds(half, half)]
        k = sum(2 * p.depth for p in self.parts[:i]) + number
        return pltpu.make_async_remote_copy(
            source,
            target,
            self.send_sem.at[k],
            self.recv_sem.at[k],
            device_id={"dp": self.partner[part.inner[level]]},
            device_id_type=pl.DeviceIdType.MESH,
        )

    def finish(self, i, number):
        self.exchange(i, number).wait()
        part = self.parts[i]
        if number < part.depth:
            half = part.shards >> (number + 1)
            at = (part.shards if part.outer else 0) + part.shards - 2 * half
            self.add(i, at, half, self.gathers[i] if number == part.depth - 1 else self.bufs[i])


def buffers(summed, gathered):
    return (
        [pltpu.VMEM((p.shards, p.each, p.cols), p.dtype) for p in summed]
        + [pltpu.VMEM((p.shards * (2 if p.outer else 1) - 1, p.each, p.cols), p.dtype) for p in summed]
        + [pltpu.VMEM((p.shards, p.each, p.cols), p.dtype) for p in gathered]
    )


def semaphores(parts):
    exchanges = sum(2 * p.depth for p in parts)
    return [
        pltpu.SemaphoreType.DMA((2 * len(parts),)),
        pltpu.SemaphoreType.DMA((len(parts),)),
        pltpu.SemaphoreType.DMA((exchanges,)),
        pltpu.SemaphoreType.DMA((exchanges,)),
    ]


def attend_back_kernel(parts, plan, slots, bits, arrays, total, *refs):
    count = len(parts)
    q_ref, k_ref, v_ref, o_ref, inverse_ref, weights_ref, branch_ref, ow_ref, att_ref, normed_ref = refs[:10]
    sources, recvs, refs = refs[10 : 10 + arrays], refs[10 + arrays : 10 + arrays + count], refs[10 + arrays + count :]
    dq_ref, dk_ref, dv_ref, dow_ref, diw_ref = refs[:5]
    results, refs = refs[5 : 5 + count], refs[5 + count :]
    dk_sum, dv_sum, g_ref = refs[:3]
    refs = refs[3:]
    sums = Reduction(
        parts, bits, refs[:count], refs[count : 2 * count], refs[2 * count : 3 * count], refs[3 * count :]
    )
    step, steps = pl.program_id(1), pl.num_programs(1)
    low_half = lax.broadcasted_iota(jnp.int32, (1, PAIR), 1) < HEAD_DIM
    zero = jnp.zeros((), BF16)
    now = pl.program_id(0) * steps + step

    @pl.when(now == 0)
    def _():
        for i in range(count):
            sums.load(i, sources[parts[i].array], recvs[i])
        sums.greet()

    def advance(i, number):
        if number == 0:
            sums.begin(i)
        else:
            sums.finish(i, number - 1)
        if number < 2 * parts[i].depth:
            sums.exchange(i, number).start()
        else:
            sums.store(i, results[i])

    places = slots or [total * k // len(plan) for k in range(len(plan))]
    for slot in sorted(set(places)):
        if slot < total:

            @pl.when(now == slot)
            def _(slot=slot):
                for event, place in zip(plan, places):
                    if place == slot:
                        advance(*event)

    @pl.when(step == 0)
    def _():
        dk_sum[...] = jnp.zeros_like(dk_sum)
        dv_sum[...] = jnp.zeros_like(dv_sum)
        branch = branch_ref[...]
        g_ref[...] = dot_nt(branch, ow_ref[...]).astype(BF16)
        dow_ref[...] = dot_tn(att_ref[...], branch).astype(BF16)

    keys, values, queries = k_ref[...], v_ref[...], q_ref[...]
    block = queries.shape[0]
    mine = pl.ds(pl.multiple_of(step * block, block), block)
    grads = (g_ref[mine, :].astype(F32) * inverse_ref[...]).astype(BF16)
    products = grads.astype(F32) * o_ref[...]
    query_grad = None
    for head in range(2):
        own = low_half if head == 0 else ~low_half
        inner = jnp.sum(jnp.where(own, products, 0.0), axis=1, keepdims=True)
        weights = weights_ref[head]
        pushed = dot_nt(grads, jnp.where(own, values, zero))
        score_grad = (weights.astype(F32) * (pushed - inner)).astype(BF16)
        part = dot_nn(score_grad, jnp.where(own, keys, zero))
        query_grad = part if query_grad is None else query_grad + part
        dv_sum[...] += dot_tn(weights, jnp.where(own, grads, zero))
        dk_sum[...] += dot_tn(score_grad, jnp.where(own, queries, zero))
    dq_ref[mine, :] = (query_grad * 0.125).astype(BF16)

    @pl.when(step == steps - 1)
    def _():
        dk_ref[...] = (dk_sum[...] * 0.125).astype(BF16)
        dv_ref[...] = dv_sum[...].astype(BF16)
        joint = jnp.concatenate([dq_ref[...], dk_ref[...], dv_ref[...]], axis=1)
        product = dot_tn(normed_ref[...], joint).astype(BF16)
        for c in range(3):
            diw_ref[c] = product[:, c * PAIR : (c + 1) * PAIR]

    @pl.when(now == total - 1)
    def _():
        for event, place in zip(plan, places):
            if place >= total:
                advance(*event)
        for i in range(count):
            sums.store_wait(i)


def attend_back(queries, keys, values, outs, inverse, weights, branch, output_weight, attended, normed, sources, recvs, plan, bits, block=224):
    parts, plan, slots = plan
    rows, width = queries.shape
    pairs = width // PAIR
    tile = pl.BlockSpec((block, PAIR), lambda p, i: (i, p))
    whole = pl.BlockSpec((rows, PAIR), lambda p, i: (0, p))
    depth = branch.shape[1]
    all_rows = pl.BlockSpec((rows, depth), lambda p, i: (0, 0), pipeline_mode=pl.Buffered(1))
    heads = pl.BlockSpec((PAIR, depth), lambda p, i: (p, 0))
    anywhere = pl.BlockSpec(memory_space=pl.ANY)
    results = pl.pallas_call(
        functools.partial(attend_back_kernel, parts, plan, slots, bits, len(sources), pairs * (rows // block)),
        grid=(pairs, rows // block),
        in_specs=[tile, whole, whole, tile, tile, pl.BlockSpec((2, block, rows), lambda p, i: (p, i, 0))]
        + [all_rows, heads, whole, all_rows]
        + [anywhere] * (len(sources) + len(recvs)),
        out_specs=[whole, whole, whole, heads, pl.BlockSpec((3, depth, PAIR), lambda p, i: (0, 0, p))]
        + [anywhere] * len(parts),
        out_shape=[jax.ShapeDtypeStruct((rows, width), BF16)] * 3
        + [jax.ShapeDtypeStruct((width, depth), BF16), jax.ShapeDtypeStruct((3, depth, width), BF16)]
        + [jax.ShapeDtypeStruct((p.half_rows, p.cols), p.dtype) for p in parts],
        scratch_shapes=[pltpu.VMEM((rows, PAIR), F32)] * 2
        + [pltpu.VMEM((rows, PAIR), BF16)]
        + buffers(parts, parts) + semaphores(parts),
        compiler_params=pltpu.CompilerParams(vmem_limit_bytes=60 << 20, collective_id=0, has_side_effects=True),
        cost_estimate=pl.CostEstimate(
            flops=16 * pairs * rows * rows * HEAD_DIM * 4,
            bytes_accessed=4 * pairs * rows * rows,
            transcendentals=0,
        ),
        name="attend_back",
    )(queries, keys, values, outs, inverse, weights, branch, output_weight, attended, normed, *sources, *recvs)
    return results[:3], results[3], results[4], results[5:]


def rest_kernel(parts, plan, bits, arrays, *refs):
    count = len(parts)
    sources, refs = refs[:arrays], refs[arrays:]
    outer = [i for i, p in enumerate(parts) if p.outer]
    recvs, refs = dict(zip(outer, refs[: len(outer)])), refs[len(outer) :]
    results, refs = refs[:count], refs[count:]
    sums = Reduction(
        parts, bits, refs[:count], refs[count : 2 * count], refs[2 * count : 3 * count], refs[3 * count :]
    )
    for i in range(count):
        sums.load(i, sources[parts[i].array], recvs.get(i))
    sums.greet()

    def advance(i, number):
        if number == 0:
            sums.begin(i)
        else:
            sums.finish(i, number - 1)
        if number < 2 * parts[i].depth:
            sums.exchange(i, number).start()
        else:
            sums.store(i, results[i])

    for event in plan:
        advance(*event)
    for i in range(count):
        sums.store_wait(i)


def rest_sums(sources, recvs, parts, plan, bits):
    anywhere = pl.BlockSpec(memory_space=pl.ANY)
    shapes = [
        jax.ShapeDtypeStruct((p.half_rows if p.outer else p.first + p.shards * p.each, p.cols), p.dtype)
        for p in parts
    ]
    return pl.pallas_call(
        functools.partial(rest_kernel, parts, plan, bits, len(sources)),
        in_specs=[anywhere] * (len(sources) + len(recvs)),
        out_specs=[anywhere] * len(shapes),
        out_shape=shapes,
        scratch_shapes=buffers(parts, parts) + semaphores(parts),
        compiler_params=pltpu.CompilerParams(vmem_limit_bytes=60 << 20, collective_id=1, has_side_effects=True),
        name="rest_sums",
    )(*sources, *recvs)


ROOT_HALF = 0.7071067811865476
HALF_LOG2E = -0.5 * 1.4426950408889634
NORMAL_PEAK = 0.3989422804014327


def column_sum(values):
    return jnp.sum(values, axis=0, dtype=F32)


def shards(
    tokens,
    attention_gain,
    attention_shift,
    input_weight,
    query_bias,
    value_bias,
    output_weight,
    output_bias,
    feedforward_gain,
    feedforward_shift,
    expand_weight,
    expand_bias,
    reduce_weight,
    reduce_bias,
    cotangent,
):
    rows = tokens.shape[0]
    cores = lax.axis_size("tensor")
    core = lax.axis_index("tensor")
    share = rows // cores
    n = lax.axis_size("dp")
    bits = n.bit_length() - 1
    orders = orders_of(bits)

    if cores == 2:

        def own_first(values):
            own = lax.dynamic_slice_in_dim(values, core * share, share, 0)
            return jnp.concatenate([own, lax.dynamic_slice_in_dim(values, (1 - core) * share, share, 0)])

        def swap(values):
            return lax.ppermute(values, "tensor", [(0, 1), (1, 0)])

        def scatter(product, values):
            other = product(*(v[share:] for v in values)).astype(BF16)
            other = swap(other)
            return product(*(v[:share] for v in values)) + other.astype(F32)

        def gather(values):
            return jnp.concatenate([values, swap(values)])

        def gather_in_order(values):
            other = swap(values)
            first = core == 0
            return jnp.concatenate([jnp.where(first, values, other), jnp.where(first, other, values)])

        first_row = 0
    else:

        def own_first(values):
            return values

        def scatter(product, values):
            return lax.psum_scatter(product(*values).astype(BF16), "tensor", scatter_dimension=0, tiled=True).astype(F32)

        def gather(values):
            return lax.all_gather(values, "tensor", axis=0, tiled=True)

        gather_in_order = gather
        first_row = core * share

    def own_rows(values):
        if cores == 2:
            return values[:share]
        return lax.dynamic_slice_in_dim(values, first_row, share, 0)

    stacked_weight = jnp.transpose(input_weight, (1, 0, 2))
    tokens = own_first(tokens)
    cotangent = own_first(cotangent)
    inputs = tokens.astype(F32)
    normed = layer_norm(inputs, attention_gain, attention_shift).astype(BF16)
    queries = (dot_nn(normed, stacked_weight[0]) + query_bias).astype(BF16)
    keys = dot_nn(normed, stacked_weight[1]).astype(BF16)
    values = (dot_nn(normed, stacked_weight[2]) + value_bias).astype(BF16)
    attended, exact, inverse, weights = attend(queries, keys, values)
    own_inputs = own_rows(tokens).astype(F32)
    middle = own_inputs + scatter(lambda part: dot_nn(part, output_weight), (attended,)) + output_bias
    normed_two = layer_norm(middle, feedforward_gain, feedforward_shift).astype(BF16)
    gathered = gather(normed_two)
    activated, hidden_grad, expand_bias_grad = feed(gathered, cotangent, expand_weight, reduce_weight, expand_bias)
    reduce_weight_grad = dot_tn(activated, cotangent).astype(BF16)
    expand_weight_grad = dot_tn(gathered, hidden_grad).astype(BF16)
    feeds = (reduce_weight_grad, expand_weight_grad)
    feed_parts, feed_steps, feed_slots = feed_plan([grad.shape for grad in feeds], n)
    gifts = [outer_gift(feeds[part.array], part) for part in feed_parts]
    hidden_grad, *gifts = lax.optimization_barrier((hidden_grad, *gifts))
    feed_recvs = [swap_bit(gift, part.order[0], n) for gift, part in zip(gifts, feed_parts)]

    normed_two_grad = scatter(lambda part: dot_nt(part, expand_weight), (hidden_grad,))
    own_upstream = own_rows(cotangent).astype(F32)
    _, second_pull = jax.vjp(layer_norm, middle, feedforward_gain, feedforward_shift)
    middle_grad, second_gain_part, second_shift_part = second_pull(normed_two_grad)
    middle_grad = middle_grad + own_upstream
    branch_grad = gather(middle_grad.astype(BF16))
    joint_grad, output_weight_grad, input_weight_grad, feed_sums = attend_back(
        queries,
        keys,
        values,
        exact,
        inverse,
        weights,
        branch_grad,
        output_weight,
        attended,
        normed,
        feeds,
        feed_recvs,
        (feed_parts, feed_steps, feed_slots),
        bits,
    )
    rest = [input_weight_grad.reshape(-1, input_weight_grad.shape[2]), output_weight_grad]
    fits = [divides(part.shape, part.dtype, n) for part in rest]
    sources = [part for part, fit in zip(rest, fits) if fit]
    rest_parts, rest_steps = rest_plan([part.shape for part in sources], n)
    gifts = [outer_gift(sources[part.array], part) for part in rest_parts]
    *joint_grad, activated, feed_sums, gifts = lax.optimization_barrier((*joint_grad, activated, feed_sums, gifts))
    rest_recvs = [swap_bit(gift, part.order[0], n) for gift, part in zip(gifts, rest_parts)]
    feed_others = [swap_bit(own, part.order[0], n) for own, part in zip(feed_sums, feed_parts)]

    def back_through(query_part, key_part, value_part):
        return (
            dot_nt(query_part, stacked_weight[0])
            + dot_nt(key_part, stacked_weight[1])
            + dot_nt(value_part, stacked_weight[2])
        )

    normed_grad = scatter(back_through, tuple(joint_grad))
    _, first_pull = jax.vjp(layer_norm, own_inputs, attention_gain, attention_shift)
    inputs_grad, first_gain_part, first_shift_part = first_pull(normed_grad)
    tokens_gradient = gather_in_order((inputs_grad + middle_grad).astype(BF16))
    update = scatter(lambda part: dot_nn(part, reduce_weight), (activated,))
    result = middle + (update + reduce_bias)
    block_out = gather_in_order(result.astype(BF16))
    norm_parts = jnp.stack([first_gain_part, first_shift_part, second_gain_part, second_shift_part])
    norm_parts = norm_parts + swap(norm_parts) if cores == 2 else lax.psum(norm_parts, "tensor")
    small = [
        norm_parts.reshape(-1),
        column_sum(cotangent),
        column_sum(branch_grad),
        column_sum(joint_grad[0]),
        column_sum(joint_grad[2]),
        expand_bias_grad,
    ]
    sizes = [part.shape[0] for part in small]
    table_rows = -(-sum(sizes) // (n * 8 * 128)) * n * 8
    table = jnp.pad(jnp.concatenate(small), (0, table_rows * 128 - sum(sizes))).reshape(table_rows, 128)
    table_parts = parts_of(len(sources), table.shape, F32, n, (1,), orders, outer=False)
    steps = list(rest_steps)
    for k in range(2 * bits, -1, -1):
        steps.insert(k * len(steps) // (2 * bits + 1), (len(rest_parts), k))
    summed = rest_sums([*sources, table], rest_recvs, rest_parts + table_parts, steps, bits)
    rest_others = [swap_bit(own, part.order[0], n) for own, part in zip(summed, rest_parts)]
    feed_sums, summed = lax.optimization_barrier((feed_sums, summed))
    reduce_total, expand_total = join(feed_parts, feed_sums, feed_others, [grad.shape for grad in feeds])
    joined = list(join(rest_parts, summed[:-1], rest_others, [part.shape for part in sources]))
    sums = [joined.pop(0) if fit else lax.psum(part, "dp").astype(F32) for part, fit in zip(rest, fits)]
    flat = summed[-1].reshape(-1)
    ends = [sum(sizes[: i + 1]) for i in range(len(sizes))]
    parts = [flat[end - size : end] for size, end in zip(sizes, ends)]
    norms = parts[0].reshape(4, -1)
    return (
        block_out,
        tokens_gradient,
        norms[0],
        norms[1],
        jnp.transpose(sums[0].reshape(input_weight_grad.shape), (1, 0, 2)),
        parts[3],
        parts[4],
        sums[1],
        parts[2],
        norms[2],
        norms[3],
        expand_total,
        parts[5],
        reduce_total,
        parts[1],
    )


def solution(mesh):
    in_specs = (
        P("dp", None),
        P(),
        P(),
        P(None, None, "tensor"),
        P("tensor"),
        P("tensor"),
        P("tensor", None),
        P(),
        P(),
        P(),
        P(None, "tensor"),
        P("tensor"),
        P("tensor", None),
        P(),
        P("dp", None),
    )
    out_specs = (
        P("dp", None),
        P("dp", None),
        P(),
        P(),
        P(None, None, "tensor"),
        P("tensor"),
        P("tensor"),
        P("tensor", None),
        P(),
        P(),
        P(),
        P(None, "tensor"),
        P("tensor"),
        P("tensor", None),
        P(),
    )

    return jax.shard_map(shards, mesh=mesh, in_specs=in_specs, out_specs=out_specs, check_vma=False)
```

profile of v0, /device:TPU:0, one launch (start us, length us, event | category | flops | bytes accessed | tf_op | source)
XLA Modules:
  0.0 500.9 jit_solution(5869929128499296670)
XLA Ops:
  0.7 1.7 constant_dynamic-slice_fusion.16
  4.9 2.6 fusion.5.refs_9_
  7.5 3.0 convolution_convert_fusion.2.k_ref.refs_1_
  10.5 3.0 add_convert_fusion.4.v_ref.refs_2_
  13.6 3.0 add_convert_fusion.5.q_ref.refs_0_
  16.6 49.2 %attend.1 = (bf16[1568,512]{1,0:T(8,128)(2,1)}, f32[1568,512]{1,0:T(8,128)}, f32[1568,512]{1,0:T(8,128)}, bf16[8,1568,1568]{2,1,0:T(8,128)(2,1)}) custom-call(bf16[1568,512]{1,0:T(8,128)(2,1)} %add_convert_fusion.5.q_ref.refs_0_, bf16[1568,512]{1,0:T(8,128)(2,1)} %convolution_convert_fusion.2.k_ref.refs_1_, bf16[1568,512]{1,0:T(8,128)(2,1)} %add_convert_fusion.4.v_ref.refs_2_), custom_call_target="tpu_custom_call" | custom-call | flops 20141047808 | bytes 39337984 | tf_op jit(solution)/shard_map/attend/pallas_call | solution.py:65
  65.9 2.3 convolution_convert_fusion.3
  68.8 3.1 collective-permute-done
  71.8 1.3 fusion.53
  73.9 1.7 add_convert_fusion.3
  76.1 2.2 constant_dynamic-slice_fusion.14
  78.3 2.1 pad_maximum_fusion.2.c_ref
  80.4 3.9 pad_maximum_fusion.1.n_ref
  84.3 21.2 %feed.1 = (bf16[1568,2048]{1,0:T(8,128)(2,1)}, bf16[1568,2048]{1,0:T(8,128)(2,1)}, f32[1,2048]{1,0:T(1,128)}) custom-call(bf16[1568,1024]{1,0:T(8,128)(2,1)} %pad_maximum_fusion.1.n_ref, bf16[1568,1024]{1,0:T(8,128)(2,1)} %pad_maximum_fusion.2.c_ref, bf16[1024,2048]{1,0:T(8,128)(2,1)} %expand_ref.1, bf16[2048,1024]{1,0:T(8,128)(2,1)} %reduce_ref.1, ...), custom_call_target="tpu_custom_call" | custom-call | flops 13153337344 | bytes 38535168 | tf_op jit(solution)/shard_map/feed/pallas_call | solution.py:113
  105.5 10.6 %convolution_convert_fusion.1.refs_10_ = bf16[2048,1024]{1,0:T(8,128)(2,1)S(1)} fusion(bf16[1568,2048]{1,0:T(8,128)(2,1)} %get-tuple-element.113, bf16[784,1024]{1,0:T(8,128)(2,1)} %copy-done.5, bf16[784,1024]{1,0:T(8,128)(2,1)S(1)} %get-tuple-element.182), kind=kOutput, calls=%fused_computation.20 | convolution fusion | flops 6585188352 | bytes 13828096 | tf_op jit(solution)/shard_map/dot_general | solution.py:36
  116.2 11.4 %convolution_convert_fusion.refs_11_ = bf16[1024,2048]{1,0:T(8,128)(2,1)S(1)} fusion(bf16[1568,2048]{1,0:T(8,128)(2,1)S(1)} %copy-done.56, bf16[784,1024]{1,0:T(8,128)(2,1)} %collective-permute-done.1, bf16[784,1024]{1,0:T(8,128)(2,1)} %add_convert_fusion.3), kind=kOutput, calls=%fused_computation.19 | convolution fusion | flops 6585188352 | bytes 13828096 | tf_op jit(solution)/shard_map/dot_general | solution.py:36
  129.8 1.3 constant_dynamic-slice_fusion.10
  131.2 1.5 copy-done.42
  132.7 3.5 fusion.26
  136.4 3.3 collective-permute-done.2
  139.7 4.3 multiply_reduce_fusion
  145.1 2.0 fusion.23
  147.5 2.9 collective-permute-start.4
  150.3 1.6 collective-permute-start.5
  151.9 1.5 collective-permute-start.8
  153.4 2.1 convert_reduce_fusion.2
  156.1 6.8 %collective-permute-done.4.refs_12_ = bf16[256,1024]{1,0:T(8,128)(2,1)} collective-permute-done((bf16[256,1024]{1,0:T(8,128)(2,1)}, bf16[256,1024]{1,0:T(8,128)(2,1)}, u32[]{:S(2)}, u32[]{:S(2)}) %collective-permute-start.4) | collective-permute-done | bytes 524320 | tf_op jit(solution)/shard_map/ppermute | solution.py:196
  162.9 1.7 collective-permute-start.7
  164.9 2.8 collective-permute-start.10
  167.7 3.9 pad_maximum_fusion.3.refs_6_
  171.7 16.3 %collective-permute-done.6.refs_14_ = bf16[256,1024]{1,0:T(8,128)(2,1)S(1)} collective-permute-done((bf16[256,1024]{1,0:T(8,128)(2,1)S(1)}, bf16[256,1024]{1,0:T(8,128)(2,1)S(1)}, u32[]{:S(2)}, u32[]{:S(2)}) %collective-permute-start.6) | collective-permute-done | bytes 524320 | tf_op jit(solution)/shard_map/ppermute | solution.py:196
  188.0 1.9 collective-permute-done.10.refs_18_
  190.7 113.3 %attend_back.1 = (bf16[1568,512]{1,0:T(8,128)(2,1)}, bf16[1568,512]{1,0:T(8,128)(2,1)}, bf16[1568,512]{1,0:T(8,128)(2,1)}, bf16[512,1024]{1,0:T(8,128)(2,1)}, bf...) custom-call(bf16[1568,512]{1,0:T(8,128)(2,1)} %add_convert_fusion.5., ...), custom_call_target="tpu_custom_call" | custom-call | flops 40282095616 | bytes 39337984 | tf_op jit(solution)/shard_map/attend_back/pallas_call | solution.py:455
  306.3 1.3 constant_dynamic-slice_fusion.2
  308.2 1.4 collective-permute-start.19
  309.7 2.2 fusion.35
  315.5 5.4 %fusion.29 = bf16[784,1024]{1,0:T(8,128)(2,1)S(1)} fusion(bf16[2048,1024]{1,0:T(8,128)(2,1)S(1)} %copy-done.43, bf16[1568,2048]{1,0:T(8,128)(2,1)} %get-tuple-element.113), kind=kOutput, calls=%fused_computation.58 | convolution fusion | flops 3289137152 | bytes 9011200 | tf_op jit(solution)/shard_map/dot_general | solution.py:28
  324.4 2.4 convert_reduce_fusion.1
  326.8 2.1 collective-permute-start.20
  328.9 2.0 fusion.10
  330.9 1.6 copy-done
  332.6 1.7 fusion.13
  334.4 7.0 %add_convert_fusion.2 = bf16[784,1024]{1,0:T(8,128)(2,1)} fusion(f32[784,1024]{1,0:T(8,128)S(1)} %copy-done.3, bf16[784,1024]{1,0:T(8,128)(2,1)S(1)} %collective-permute-done.11, f32[1024]{0:T(1024)S(1)} %copy-done.51, bf16[2048,1024]{1,0:T(8,128)(2,1)S(1)} %copy-done.43, bf16[1568,2048]{1,0:T(8,128)(2,1)} %get-tuple-element.113), kind=kOutput, calls=%fused_computation.38 | convolution fusion | flops 3292348416 | bytes 13832192 | tf_op jit(solution)/shard_map/dot_general | solution.py:28
  342.1 1.5 collective-permute-start.21
  344.1 1.5 collective-permute-start.30
  345.8 15.5 %collective-permute-done.21.refs_8_ = bf16[128,1024]{1,0:T(8,128)(2,1)S(1)} collective-permute-done((bf16[128,1024]{1,0:T(8,128)(2,1)S(1)}, bf16[128,1024]{1,0:T(8,128)(2,1)S(1)}, u32[]{:S(2)}, u32[]{:S(2)}) %collective-permute-start.21) | collective-permute-done | bytes 262176 | tf_op jit(solution)/shard_map/ppermute | solution.py:196
  362.4 1.5 collective-permute-start.35
  363.9 1.5 collective-permute-start.34
  366.9 74.1 %rest_sums.1 = (bf16[256,512]{1,0:T(8,128)(2,1)}, bf16[256,512]{1,0:T(8,128)(2,1)}, bf16[512,512]{1,0:T(8,128)(2,1)}, bf16[256,512]{1,0:T(8,128)(2,1)}, bf16[256...) custom-call(bf16[3072,512]{1,0:T(8,128)(2,1)} %bitcast.65, ...), custom_call_target="tpu_custom_call" | custom-call | tf_op jit(solution)/shard_map/rest_sums/pallas_call | solution.py:515
  441.0 2.6 collective-permute-start.36
  444.4 3.3 collective-permute-start.24
  447.6 4.5 add_convert_fusion
  452.1 12.3 %collective-permute-done.36.refs_13_ = bf16[128,2048]{1,0:T(8,128)(2,1)} collective-permute-done((bf16[128,2048]{1,0:T(8,128)(2,1)}, bf16[128,2048]{1,0:T(8,128)(2,1)}, u32[]{:S(2)}, u32[]{:S(2)}) %collective-permute-start.36) | collective-permute-done | bytes 524320 | tf_op jit(solution)/shard_map/ppermute | solution.py:196
  465.5 1.3 slice_bitcast_fusion.12
  466.8 6.4 %collective-permute-done.26.refs_7_ = bf16[256,512]{1,0:T(8,128)(2,1)S(1)} collective-permute-done((bf16[256,512]{1,0:T(8,128)(2,1)S(1)}, bf16[256,512]{1,0:T(8,128)(2,1)S(1)}, u32[]{:S(2)}, u32[]{:S(2)}) %collective-permute-start.26) | collective-permute-done | bytes 262176 | tf_op jit(solution)/shard_map/ppermute | solution.py:196
  473.9 1.3 collective-permute-start.29
  475.2 1.3 slice_bitcast_fusion.19
  476.5 8.2 %join.3 = (f32[2048,1024]{1,0:T(8,128)}, f32[1024,2048]{1,0:T(8,128)}) custom-call(bf16[256,1024]{1,0:T(8,128)(2,1)} %get-tuple-element.150.refs_0_, bf16[256,1024]{1,0:T(8,128)(2,1)} %copy-done.17, bf16[256,1024]{1,0:T(8,128)(2,1)} %get-tuple-element.151.refs_2_, bf16[256,1024]{1,0:T(8,128)(2,1)} %copy-done.18, ...), custom_call_target="tpu_custom_call" | custom-call | flops 4194304 | bytes 25165824 | tf_op jit(solution)/shard_map/join/pallas_call | solution.py:236
  484.7 1.3 slice_bitcast_fusion.13
  487.7 4.5 join.2
  492.2 2.1 broadcast_select_fusion.3
  494.3 2.0 pad_maximum_fusion.4
  496.3 2.1 broadcast_select_fusion.1
  498.4 2.0 pad_maximum_fusion.5
  (196 shorter events, 28.0 us)
Async XLA Ops:
  7.5 6.1 %copy-start.8 = (bf16[1568,1024]{1,0:T(8,128)(2,1)}, bf16[1568,1024]{1,0:T(8,128)(2,1)S(1)}, u32[]{:S(2)}) copy-start(bf16[1568,1024]{1,0:T(8,128)(2,1)S(1)} %fusion.5.refs_9_) | copy-start | bytes 9633796
  16.6 49.3 %copy-start.44 = (bf16[512,1024]{1,0:T(8,128)(2,1)S(1)}, bf16[512,1024]{1,0:T(8,128)(2,1)}, u32[]{:S(2)}) copy-start(bf16[512,1024]{1,0:T(8,128)(2,1)} %refs_7_.1) | copy-start | bytes 3145732
  65.9 6.0 %copy-start.45 = (bf16[512,1024]{1,0:T(8,128)(2,1)S(1)}, bf16[512,1024]{1,0:T(8,128)(2,1)}, u32[]{:S(2)}) copy-start(bf16[512,1024]{1,0:T(8,128)(2,1)} %refs_7_.1) | copy-start | bytes 3145732
  65.9 6.0 %copy-start.50 = (f32[1024]{0:T(1024)S(1)}, f32[1024]{0:T(1024)}, u32[]{:S(2)}) copy-start(f32[1024]{0:T(1024)} %param.22) | copy-start | bytes 12292
  65.9 6.0 %copy-start.55 = (bf16[1568,512]{1,0:T(8,128)(2,1)S(1)}, bf16[1568,512]{1,0:T(8,128)(2,1)}, u32[]{:S(2)}) copy-start(bf16[1568,512]{1,0:T(8,128)(2,1)} %get-tuple-element.87.refs_8_) | copy-start | bytes 4816900
  68.2 3.6 collective-permute-start
  75.7 4.7 collective-permute-start.1
  105.5 10.7 %copy-start.56 = (bf16[1568,2048]{1,0:T(8,128)(2,1)S(1)}, bf16[1568,2048]{1,0:T(8,128)(2,1)}, u32[]{:S(2)}) copy-start(bf16[1568,2048]{1,0:T(8,128)(2,1)} %get-tuple-element.93) | copy-start | bytes 19267588
  116.2 13.6 %copy-start.13 = (bf16[2048,1024]{1,0:T(8,128)(2,1)}, bf16[2048,1024]{1,0:T(8,128)(2,1)S(1)}, u32[]{:S(2)}) copy-start(bf16[2048,1024]{1,0:T(8,128)(2,1)S(1)} %convolution_convert_fusion.1.refs_10_) | copy-start | bytes 12582916
  128.7 3.9 copy-start.42
  132.7 7.0 %copy-start.2 = (f32[784,1024]{1,0:T(8,128)S(1)}, f32[784,1024]{1,0:T(8,128)}, u32[]{:S(2)}) copy-start(f32[784,1024]{1,0:T(8,128)} %copy-done.1) | copy-start | bytes 9633796
  136.2 3.5 collective-permute-start.2
  147.3 17.6 %collective-permute-start.3 = (bf16[784,1024]{1,0:T(8,128)(2,1)}, bf16[784,1024]{1,0:T(8,128)(2,1)}, u32[]{:S(2)}, u32[]{:S(2)}) collective-permute-start(bf16[784,1024]{1,0:T(8,128)(2,1)} %fusion.23), channel_id=1, source_target_pairs={{0,1},{1,0},{2,3},{3,2},{4,5},{5,4},{6,7},{7,6},{8,9},{9,8},{10,11... | collective-permute-start | bytes 4816904 | tf_op jit(solution)/shard_map/ppermute | solution.py:567
  147.5 15.4 %collective-permute-start.4 = (bf16[256,1024]{1,0:T(8,128)(2,1)}, bf16[256,1024]{1,0:T(8,128)(2,1)}, u32[]{:S(2)}, u32[]{:S(2)}) collective-permute-start(bf16[256,1024]{1,0:T(8,128)(2,1)} %get-tuple-element.94), channel_id=1, source_target_pairs={{0,4},{2,6},{4,0},{6,2},{8,12},{10,14},{12,8},{14,10},{16,20},{18,... | collective-permute-start | bytes 1572872 | tf_op jit(solution)/shard_map/ppermute | solution.py:196
  150.3 14.3 %collective-permute-start.5 = (bf16[256,1024]{1,0:T(8,128)(2,1)}, bf16[256,1024]{1,0:T(8,128)(2,1)}, u32[]{:S(2)}, u32[]{:S(2)}) collective-permute-start(bf16[256,1024]{1,0:T(8,128)(2,1)} %get-tuple-element.95), channel_id=1, source_target_pairs={{0,8},{2,10},{4,12},{6,14},{8,0},{10,2},{12,4},{14,6},{16,24},{18,... | collective-permute-start | bytes 1572872 | tf_op jit(solution)/shard_map/ppermute | solution.py:196
  151.9 38.0 %collective-permute-start.8 = (bf16[256,2048]{1,0:T(8,128)(2,1)}, bf16[256,2048]{1,0:T(8,128)(2,1)}, u32[]{:S(2)}, u32[]{:S(2)}) collective-permute-start(bf16[256,2048]{1,0:T(8,128)(2,1)} %constant_dynamic-slice_fusion.9), channel_id=1, source_target_pairs={{0,2},{2,0},{4,6},{6,4},{8,10},{10,8},{12,14},{14,12},{16,18},{18,... | collective-permute-start | bytes 3145736 | tf_op jit(solution)/shard_map/ppermute | solution.py:196
  153.4 9.5 %copy-start.22 = (bf16[256,1024]{1,0:T(8,128)(2,1)S(1)}, bf16[256,1024]{1,0:T(8,128)(2,1)}, u32[]{:S(2)}) copy-start(bf16[256,1024]{1,0:T(8,128)(2,1)} %get-tuple-element.97) | copy-start | bytes 1572868
  153.4 11.2 %copy-start.21 = (bf16[128,2048]{1,0:T(8,128)(2,1)S(1)}, bf16[128,2048]{1,0:T(8,128)(2,1)}, u32[]{:S(2)}) copy-start(bf16[128,2048]{1,0:T(8,128)(2,1)} %get-tuple-element.99) | copy-start | bytes 1572868
  153.4 11.5 %copy-start.20 = (bf16[128,2048]{1,0:T(8,128)(2,1)S(1)}, bf16[128,2048]{1,0:T(8,128)(2,1)}, u32[]{:S(2)}) copy-start(bf16[128,2048]{1,0:T(8,128)(2,1)} %get-tuple-element.100) | copy-start | bytes 1572868
  155.5 32.5 %collective-permute-start.6 = (bf16[256,1024]{1,0:T(8,128)(2,1)S(1)}, bf16[256,1024]{1,0:T(8,128)(2,1)S(1)}, u32[]{:S(2)}, u32[]{:S(2)}) collective-permute-start(bf16[256,1024]{1,0:T(8,128)(2,1)S(1)} %copy-done.23), channel_id=1, source_target_pairs={{0,2},{2,0},{4,6},{6,4},{8,10},{10,8},{12,14},{14,12},{16,18},{18,... | collective-permute-start | bytes 1572872 | tf_op jit(solution)/shard_map/ppermute | solution.py:196
  162.9 25.1 %collective-permute-start.7 = (bf16[256,1024]{1,0:T(8,128)(2,1)S(1)}, bf16[256,1024]{1,0:T(8,128)(2,1)S(1)}, u32[]{:S(2)}, u32[]{:S(2)}) collective-permute-start(bf16[256,1024]{1,0:T(8,128)(2,1)S(1)} %copy-done.22), channel_id=1, source_target_pairs={{0,4},{2,6},{4,0},{6,2},{8,12},{10,14},{12,8},{14,10},{16,20},{18,... | collective-permute-start | bytes 1572872 | tf_op jit(solution)/shard_map/ppermute | solution.py:196
  164.6 23.4 %collective-permute-start.9 = (bf16[128,2048]{1,0:T(8,128)(2,1)S(1)}, bf16[128,2048]{1,0:T(8,128)(2,1)S(1)}, u32[]{:S(2)}, u32[]{:S(2)}) collective-permute-start(bf16[128,2048]{1,0:T(8,128)(2,1)S(1)} %copy-done.21), channel_id=1, source_target_pairs={{0,4},{2,6},{4,0},{6,2},{8,12},{10,14},{12,8},{14,10},{16,20},{18,... | collective-permute-start | bytes 1572872 | tf_op jit(solution)/shard_map/ppermute | solution.py:196
  164.9 25.0 %collective-permute-start.10 = (bf16[128,2048]{1,0:T(8,128)(2,1)S(1)}, bf16[128,2048]{1,0:T(8,128)(2,1)S(1)}, u32[]{:S(2)}, u32[]{:S(2)}) collective-permute-start(bf16[128,2048]{1,0:T(8,128)(2,1)S(1)} %copy-done.20), channel_id=1, source_target_pairs={{0,16},{2,18},{4,20},{6,22},{8,24},{10,26},{12,28},{14,30},{16,0},... | collective-permute-start | bytes 1572872 | tf_op jit(solution)/shard_map/ppermute | solution.py:196
  304.0 5.7 %copy-start.11 = (bf16[1024,3,512]{2,0,1:T(8,128)(2,1)S(1)}, bf16[1024,3,512]{2,0,1:T(8,128)(2,1)}, u32[]{:S(2)}) copy-start(bf16[1024,3,512]{2,0,1:T(8,128)(2,1)} %param.18) | copy-start | bytes 9437188
  307.6 4.3 copy-start.9
  307.6 34.5 %collective-permute-start.16 = (bf16[256,512]{1,0:T(8,128)(2,1)S(1)}, bf16[256,512]{1,0:T(8,128)(2,1)S(1)}, u32[]{:S(2)}, u32[]{:S(2)}) collective-permute-start(bf16[256,512]{1,0:T(8,128)(2,1)S(1)} %get-tuple-element.125), channel_id=1, source_target_pairs={{0,4},{2,6},{4,0},{6,2},{8,12},{10,14},{12,8},{14,10},{16,20},{18,... | collective-permute-start | bytes 786440 | tf_op jit(solution)/shard_map/ppermute | solution.py:196
  308.2 35.3 %collective-permute-start.17 = (bf16[256,512]{1,0:T(8,128)(2,1)S(1)}, bf16[256,512]{1,0:T(8,128)(2,1)S(1)}, u32[]{:S(2)}, u32[]{:S(2)}) collective-permute-start(bf16[256,512]{1,0:T(8,128)(2,1)S(1)} %get-tuple-element.126), channel_id=1, source_target_pairs={{0,8},{2,10},{4,12},{6,14},{8,0},{10,2},{12,4},{14,6},{16,24},{18,... | collective-permute-start | bytes 786440 | tf_op jit(solution)/shard_map/ppermute | solution.py:196
  308.2 35.9 %collective-permute-start.19 = (bf16[256,512]{1,0:T(8,128)(2,1)S(1)}, bf16[256,512]{1,0:T(8,128)(2,1)S(1)}, u32[]{:S(2)}, u32[]{:S(2)}) collective-permute-start(bf16[256,512]{1,0:T(8,128)(2,1)S(1)} %get-tuple-element.128), channel_id=1, source_target_pairs={{0,4},{2,6},{4,0},{6,2},{8,12},{10,14},{12,8},{14,10},{16,20},{18,... | collective-permute-start | bytes 786440 | tf_op jit(solution)/shard_map/ppermute | solution.py:196
  314.3 12.5 %collective-permute-start.13 = (bf16[784,1024]{1,0:T(8,128)(2,1)S(1)}, bf16[784,1024]{1,0:T(8,128)(2,1)S(1)}, u32[]{:S(2)}, u32[]{:S(2)}) collective-permute-start(bf16[784,1024]{1,0:T(8,128)(2,1)S(1)} %add_convert_fusion.1), channel_id=1, source_target_pairs={{0,1},{1,0},{2,3},{3,2},{4,5},{5,4},{6,7},{7,6},{8,9},{9,8},{10,11... | collective-permute-start | bytes 4816904 | tf_op jit(solution)/shard_map/ppermute | solution.py:567
  320.9 13.4 %collective-permute-start.11 = (bf16[784,1024]{1,0:T(8,128)(2,1)S(1)}, bf16[784,1024]{1,0:T(8,128)(2,1)S(1)}, u32[]{:S(2)}, u32[]{:S(2)}) collective-permute-start(bf16[784,1024]{1,0:T(8,128)(2,1)S(1)} %fusion.29), channel_id=1, source_target_pairs={{0,1},{1,0},{2,3},{3,2},{4,5},{5,4},{6,7},{7,6},{8,9},{9,8},{10,11... | collective-permute-start | bytes 4816904 | tf_op jit(solution)/shard_map/ppermute | solution.py:567
  324.4 4.5 copy-start.37
  326.8 18.8 %collective-permute-start.20 = (bf16[256,512]{1,0:T(8,128)(2,1)S(1)}, bf16[256,512]{1,0:T(8,128)(2,1)S(1)}, u32[]{:S(2)}, u32[]{:S(2)}) collective-permute-start(bf16[256,512]{1,0:T(8,128)(2,1)S(1)} %get-tuple-element.129), channel_id=1, source_target_pairs={{0,8},{2,10},{4,12},{6,14},{8,0},{10,2},{12,4},{14,6},{16,24},{18,... | collective-permute-start | bytes 786440 | tf_op jit(solution)/shard_map/ppermute | solution.py:196
  334.3 9.9 %copy-start.14 = (bf16[256,1024]{1,0:T(8,128)(2,1)S(1)}, bf16[256,1024]{1,0:T(8,128)(2,1)}, u32[]{:S(2)}) copy-start(bf16[256,1024]{1,0:T(8,128)(2,1)} %get-tuple-element.150.refs_0_) | copy-start | bytes 1572868
  334.3 11.4 %copy-start.15 = (bf16[256,1024]{1,0:T(8,128)(2,1)S(1)}, bf16[256,1024]{1,0:T(8,128)(2,1)}, u32[]{:S(2)}) copy-start(bf16[256,1024]{1,0:T(8,128)(2,1)} %get-tuple-element.151.refs_2_) | copy-start | bytes 1572868
  334.3 27.0 %copy-start.16 = (bf16[256,1024]{1,0:T(8,128)(2,1)S(1)}, bf16[256,1024]{1,0:T(8,128)(2,1)}, u32[]{:S(2)}) copy-start(bf16[256,1024]{1,0:T(8,128)(2,1)} %get-tuple-element.152.refs_4_) | copy-start | bytes 1572868
  334.3 31.1 %copy-start.39 = (f32[1,2048]{1,0:T(1,128)S(1)}, f32[1,2048]{1,0:T(1,128)}, u32[]{:S(2)}) copy-start(f32[1,2048]{1,0:T(1,128)} %get-tuple-element.124) | copy-start | bytes 24580
  334.3 7.1 %collective-permute-start.15 = (f32[4,1024]{1,0:T(4,128)S(1)}, f32[4,1024]{1,0:T(4,128)S(1)}, u32[]{:S(2)}, u32[]{:S(2)}) collective-permute-start(f32[4,1024]{1,0:T(4,128)S(1)} %pad_maximum_fusion.6), channel_id=1, source_target_pairs={{0,1},{1,0},{2,3},{3,2},{4,5},{5,4},{6,7},{7,6},{8,9},{9,8},{10,11... | collective-permute-start | bytes 49160 | tf_op jit(solution)/shard_map/ppermute | solution.py:567
  341.4 21.0 %collective-permute-start.18 = (bf16[512,512]{1,0:T(8,128)(2,1)S(1)}, bf16[512,512]{1,0:T(8,128)(2,1)S(1)}, u32[]{:S(2)}, u32[]{:S(2)}) collective-permute-start(bf16[512,512]{1,0:T(8,128)(2,1)S(1)} %constant_dynamic-slice_fusion.4), channel_id=1, source_target_pairs={{0,2},{2,0},{4,6},{6,4},{8,10},{10,8},{12,14},{14,12},{16,18},{18,... | collective-permute-start | bytes 1572872 | tf_op jit(solution)/shard_map/ppermute | solution.py:196
  342.1 24.8 %copy-start.25 = (bf16[256,512]{1,0:T(8,128)(2,1)}, bf16[256,512]{1,0:T(8,128)(2,1)S(1)}, u32[]{:S(2)}) copy-start(bf16[256,512]{1,0:T(8,128)(2,1)S(1)} %collective-permute-done.16.refs_3_) | copy-start | bytes 786436
  342.1 19.2 %collective-permute-start.21 = (bf16[128,1024]{1,0:T(8,128)(2,1)S(1)}, bf16[128,1024]{1,0:T(8,128)(2,1)S(1)}, u32[]{:S(2)}, u32[]{:S(2)}) collective-permute-start(bf16[128,1024]{1,0:T(8,128)(2,1)S(1)} %get-tuple-element.130), channel_id=1, source_target_pairs={{0,2},{2,0},{4,6},{6,4},{8,10},{10,8},{12,14},{14,12},{16,18},{18,... | collective-permute-start | bytes 786440 | tf_op jit(solution)/shard_map/ppermute | solution.py:196
  343.6 22.0 %copy-start.26 = (bf16[256,512]{1,0:T(8,128)(2,1)}, bf16[256,512]{1,0:T(8,128)(2,1)S(1)}, u32[]{:S(2)}) copy-start(bf16[256,512]{1,0:T(8,128)(2,1)S(1)} %collective-permute-done.17.refs_4_) | copy-start | bytes 786436
  343.6 18.3 %collective-permute-start.22 = (bf16[128,1024]{1,0:T(8,128)(2,1)S(1)}, bf16[128,1024]{1,0:T(8,128)(2,1)S(1)}, u32[]{:S(2)}, u32[]{:S(2)}) collective-permute-start(bf16[128,1024]{1,0:T(8,128)(2,1)S(1)} %get-tuple-element.131), channel_id=1, source_target_pairs={{0,4},{2,6},{4,0},{6,2},{8,12},{10,14},{12,8},{14,10},{16,20},{18,... | collective-permute-start | bytes 786440 | tf_op jit(solution)/shard_map/ppermute | solution.py:196
  344.1 21.4 %copy-start.27 = (bf16[256,512]{1,0:T(8,128)(2,1)}, bf16[256,512]{1,0:T(8,128)(2,1)S(1)}, u32[]{:S(2)}) copy-start(bf16[256,512]{1,0:T(8,128)(2,1)S(1)} %collective-permute-done.19.refs_6_) | copy-start | bytes 786436
  344.1 19.8 %collective-permute-start.30 = (bf16[256,1024]{1,0:T(8,128)(2,1)S(1)}, bf16[256,1024]{1,0:T(8,128)(2,1)S(1)}, u32[]{:S(2)}, u32[]{:S(2)}) collective-permute-start(bf16[256,1024]{1,0:T(8,128)(2,1)S(1)} %copy-done.14), channel_id=1, source_target_pairs={{0,4},{2,6},{4,0},{6,2},{8,12},{10,14},{12,8},{14,10},{16,20},{18,... | collective-permute-start | bytes 1572872 | tf_op jit(solution)/shard_map/ppermute | solution.py:196
  345.7 19.9 %copy-start.28 = (bf16[256,512]{1,0:T(8,128)(2,1)}, bf16[256,512]{1,0:T(8,128)(2,1)S(1)}, u32[]{:S(2)}) copy-start(bf16[256,512]{1,0:T(8,128)(2,1)S(1)} %collective-permute-done.20.refs_7_) | copy-start | bytes 786436
  345.7 19.8 %collective-permute-start.31 = (bf16[256,1024]{1,0:T(8,128)(2,1)S(1)}, bf16[256,1024]{1,0:T(8,128)(2,1)S(1)}, u32[]{:S(2)}, u32[]{:S(2)}) collective-permute-start(bf16[256,1024]{1,0:T(8,128)(2,1)S(1)} %copy-done.15), channel_id=1, source_target_pairs={{0,8},{2,10},{4,12},{6,14},{8,0},{10,2},{12,4},{14,6},{16,24},{18,... | collective-permute-start | bytes 1572872 | tf_op jit(solution)/shard_map/ppermute | solution.py:196
  361.3 4.3 copy-start.30
  361.3 79.7 %collective-permute-start.32 = (bf16[256,1024]{1,0:T(8,128)(2,1)S(1)}, bf16[256,1024]{1,0:T(8,128)(2,1)}, u32[]{:S(2)}, u32[]{:S(2)}) collective-permute-start(bf16[256,1024]{1,0:T(8,128)(2,1)S(1)} %copy-done.16), channel_id=1, source_target_pairs={{0,2},{2,0},{4,6},{6,4},{8,10},{10,8},{12,14},{14,12},{16,18},{18,... | collective-permute-start | bytes 1572872 | tf_op jit(solution)/shard_map/ppermute | solution.py:196
  361.9 81.7 %collective-permute-start.33 = (bf16[256,1024]{1,0:T(8,128)(2,1)}, bf16[256,1024]{1,0:T(8,128)(2,1)}, u32[]{:S(2)}, u32[]{:S(2)}) collective-permute-start(bf16[256,1024]{1,0:T(8,128)(2,1)} %get-tuple-element.153.refs_6_), channel_id=1, source_target_pairs={{0,4},{2,6},{4,0},{6,2},{8,12},{10,14},{12,8},{14,10},{16,20},{18,... | collective-permute-start | bytes 1572872 | tf_op jit(solution)/shard_map/ppermute | solution.py:196
  362.4 81.9 %collective-permute-start.35 = (bf16[128,2048]{1,0:T(8,128)(2,1)}, bf16[128,2048]{1,0:T(8,128)(2,1)}, u32[]{:S(2)}, u32[]{:S(2)}) collective-permute-start(bf16[128,2048]{1,0:T(8,128)(2,1)} %get-tuple-element.155.refs_10_), channel_id=1, source_target_pairs={{0,4},{2,6},{4,0},{6,2},{8,12},{10,14},{12,8},{14,10},{16,20},{18,... | collective-permute-start | bytes 1572872 | tf_op jit(solution)/shard_map/ppermute | solution.py:196
  363.9 100.6 %collective-permute-start.34 = (bf16[256,2048]{1,0:T(8,128)(2,1)}, bf16[256,2048]{1,0:T(8,128)(2,1)}, u32[]{:S(2)}, u32[]{:S(2)}) collective-permute-start(bf16[256,2048]{1,0:T(8,128)(2,1)} %get-tuple-element.154.refs_8_), channel_id=1, source_target_pairs={{0,2},{2,0},{4,6},{6,4},{8,10},{10,8},{12,14},{14,12},{16,18},{18,... | collective-permute-start | bytes 3145736 | tf_op jit(solution)/shard_map/ppermute | solution.py:196
  365.5 126.7 %collective-permute-start.12 = (bf16[784,1024]{1,0:T(8,128)(2,1)}, bf16[784,1024]{1,0:T(8,128)(2,1)}, u32[]{:S(2)}, u32[]{:S(2)}) collective-permute-start(bf16[784,1024]{1,0:T(8,128)(2,1)} %add_convert_fusion.2), channel_id=1, source_target_pairs={{0,1},{1,0},{2,3},{3,2},{4,5},{5,4},{6,7},{7,6},{8,9},{9,8},{10,11... | collective-permute-start | bytes 4816904 | tf_op jit(solution)/shard_map/ppermute | solution.py:567
  441.0 23.5 %collective-permute-start.36 = (bf16[128,2048]{1,0:T(8,128)(2,1)}, bf16[128,2048]{1,0:T(8,128)(2,1)}, u32[]{:S(2)}, u32[]{:S(2)}) collective-permute-start(bf16[128,2048]{1,0:T(8,128)(2,1)} %get-tuple-element.156.refs_12_), channel_id=1, source_target_pairs={{0,16},{2,18},{4,20},{6,22},{8,24},{10,26},{12,28},{14,30},{16,0},... | collective-permute-start | bytes 1572872 | tf_op jit(solution)/shard_map/ppermute | solution.py:196
  443.6 21.4 %collective-permute-start.23 = (bf16[256,512]{1,0:T(8,128)(2,1)}, bf16[256,512]{1,0:T(8,128)(2,1)}, u32[]{:S(2)}, u32[]{:S(2)}) collective-permute-start(bf16[256,512]{1,0:T(8,128)(2,1)} %get-tuple-element.141.refs_0_), channel_id=1, source_target_pairs={{0,4},{2,6},{4,0},{6,2},{8,12},{10,14},{12,8},{14,10},{16,20},{18,... | collective-permute-start | bytes 786440 | tf_op jit(solution)/shard_map/ppermute | solution.py:196
  444.4 20.2 %copy-start.29 = (bf16[256,512]{1,0:T(8,128)(2,1)S(1)}, bf16[256,512]{1,0:T(8,128)(2,1)}, u32[]{:S(2)}) copy-start(bf16[256,512]{1,0:T(8,128)(2,1)} %get-tuple-element.144.refs_6_) | copy-start | bytes 786436
  444.4 20.6 %collective-permute-start.24 = (bf16[256,512]{1,0:T(8,128)(2,1)}, bf16[256,512]{1,0:T(8,128)(2,1)}, u32[]{:S(2)}, u32[]{:S(2)}) collective-permute-start(bf16[256,512]{1,0:T(8,128)(2,1)} %get-tuple-element.142.refs_2_), channel_id=1, source_target_pairs={{0,8},{2,10},{4,12},{6,14},{8,0},{10,2},{12,4},{14,6},{16,24},{18,... | collective-permute-start | bytes 786440 | tf_op jit(solution)/shard_map/ppermute | solution.py:196
  464.5 31.8 %collective-permute-start.14 = (bf16[784,1024]{1,0:T(8,128)(2,1)}, bf16[784,1024]{1,0:T(8,128)(2,1)}, u32[]{:S(2)}, u32[]{:S(2)}) collective-permute-start(bf16[784,1024]{1,0:T(8,128)(2,1)} %add_convert_fusion), channel_id=1, source_target_pairs={{0,1},{1,0},{2,3},{3,2},{4,5},{5,4},{6,7},{7,6},{8,9},{9,8},{10,11... | collective-permute-start | bytes 4816904 | tf_op jit(solution)/shard_map/ppermute | solution.py:567
  464.5 8.7 %collective-permute-start.26 = (bf16[256,512]{1,0:T(8,128)(2,1)S(1)}, bf16[256,512]{1,0:T(8,128)(2,1)S(1)}, u32[]{:S(2)}, u32[]{:S(2)}) collective-permute-start(bf16[256,512]{1,0:T(8,128)(2,1)S(1)} %copy-done.29), channel_id=1, source_target_pairs={{0,4},{2,6},{4,0},{6,2},{8,12},{10,14},{12,8},{14,10},{16,20},{18,... | collective-permute-start | bytes 786440 | tf_op jit(solution)/shard_map/ppermute | solution.py:196
  465.0 8.9 %collective-permute-start.27 = (bf16[256,512]{1,0:T(8,128)(2,1)}, bf16[256,512]{1,0:T(8,128)(2,1)S(1)}, u32[]{:S(2)}, u32[]{:S(2)}) collective-permute-start(bf16[256,512]{1,0:T(8,128)(2,1)} %get-tuple-element.145.refs_8_), channel_id=1, source_target_pairs={{0,8},{2,10},{4,12},{6,14},{8,0},{10,2},{12,4},{14,6},{16,24},{18,... | collective-permute-start | bytes 786440 | tf_op jit(solution)/shard_map/ppermute | solution.py:196
  465.0 21.1 %collective-permute-start.25 = (bf16[512,512]{1,0:T(8,128)(2,1)}, bf16[512,512]{1,0:T(8,128)(2,1)S(1)}, u32[]{:S(2)}, u32[]{:S(2)}) collective-permute-start(bf16[512,512]{1,0:T(8,128)(2,1)} %get-tuple-element.143.refs_4_), channel_id=1, source_target_pairs={{0,2},{2,0},{4,6},{6,4},{8,10},{10,8},{12,14},{14,12},{16,18},{18,... | collective-permute-start | bytes 1572872 | tf_op jit(solution)/shard_map/ppermute | solution.py:196
  473.2 11.5 %copy-start.32 = (bf16[256,512]{1,0:T(8,128)(2,1)}, bf16[256,512]{1,0:T(8,128)(2,1)S(1)}, u32[]{:S(2)}) copy-start(bf16[256,512]{1,0:T(8,128)(2,1)S(1)} %collective-permute-done.26.refs_7_) | copy-start | bytes 786436
  473.2 12.8 %collective-permute-start.28 = (bf16[128,1024]{1,0:T(8,128)(2,1)}, bf16[128,1024]{1,0:T(8,128)(2,1)S(1)}, u32[]{:S(2)}, u32[]{:S(2)}) collective-permute-start(bf16[128,1024]{1,0:T(8,128)(2,1)} %get-tuple-element.146.refs_10_), channel_id=1, source_target_pairs={{0,2},{2,0},{4,6},{6,4},{8,10},{10,8},{12,14},{14,12},{16,18},{18,... | collective-permute-start | bytes 786440 | tf_op jit(solution)/shard_map/ppermute | solution.py:196
  473.9 10.8 %copy-start.33 = (bf16[256,512]{1,0:T(8,128)(2,1)}, bf16[256,512]{1,0:T(8,128)(2,1)S(1)}, u32[]{:S(2)}) copy-start(bf16[256,512]{1,0:T(8,128)(2,1)S(1)} %collective-permute-done.27.refs_9_) | copy-start | bytes 786436
  473.9 12.2 %collective-permute-start.29 = (bf16[128,1024]{1,0:T(8,128)(2,1)}, bf16[128,1024]{1,0:T(8,128)(2,1)S(1)}, u32[]{:S(2)}, u32[]{:S(2)}) collective-permute-start(bf16[128,1024]{1,0:T(8,128)(2,1)} %get-tuple-element.147.refs_12_), channel_id=1, source_target_pairs={{0,4},{2,6},{4,0},{6,2},{8,12},{10,14},{12,8},{14,10},{16,20},{18,... | collective-permute-start | bytes 786440 | tf_op jit(solution)/shard_map/ppermute | solution.py:196
  (30 other events, 60.6 us)
where the time goes:
time: 511 us; the launch traced here: 501 us
  Pallas kernels  270 us (53%)
  waiting for transfers between devices  65.6 us (13%)
  matrix products  63.2 us (12%)
  other arithmetic  39 us (8%)
  starting transfers between devices  35.2 us (7%)
  local copies, waits for them, and re-layouts  25.4 us (5%)
    pallas_call x1, Pallas kernels, attend_back(): pl.pallas_call(functools.partial(attend_back_kernel, parts, plan, slots,...  113 us
    pallas_call x1, Pallas kernels, rest_sums(): pl.pallas_call(functools.partial(rest_kernel, parts, plan, bits, len(sour...  74.1 us
    ppermute x28, waiting for transfers between devices, swap_bit(): return lax.ppermute(values, 'dp', [(j, j ^ 1 << bit) for j in range(n)])  59.2 us
    pallas_call x1, Pallas kernels, attend(): pl.pallas_call(attend_kernel, grid=(pairs, rows // block), in_specs=[tile...  49.2 us
    ppermute x28, starting transfers between devices, swap_bit(): return lax.ppermute(values, 'dp', [(j, j ^ 1 << bit) for j in range(n)])  33.6 us
    dot_general x7, matrix products, dot_nn(): lax.dot_general(a, b, (((1,), (0,)), ((), ())), preferred_element_type=F32)  25.1 us
    dot_general x2, matrix products, dot_tn(): lax.dot_general(a, b, (((0,), (0,)), ((), ())), preferred_element_type=F32)  22 us
    pallas_call x1, Pallas kernels, feed(): pl.pallas_call(functools.partial(feed_kernel, chunk=chunk), grid=(rows //...  21.2 us
  transfers between devices with their start and end apart: 37, of which 8 were waited for; matrix products, arithmetic and copies ran while one was open for 10% of the time, Pallas kernels for 17%

commit v1 on v0

--- a/solution.py
+++ b/solution.py
@@ -40,16 +40,16 @@
     low_half = lax.broadcasted_iota(jnp.int32, (1, PAIR), 1) < HEAD_DIM
     zero = jnp.zeros((), BF16)
     keys, values, queries = k_ref[...], v_ref[...], q_ref[...]
+    values = jnp.concatenate([values, jnp.ones_like(values)], axis=1)
+    scores = [dot_nt(queries, jnp.where(own, keys, zero)) for own in (low_half, ~low_half)]
     mixed, inverses = [], []
     for head in range(2):
-        own_keys = jnp.where(low_half if head == 0 else ~low_half, keys, zero)
-        scores = dot_nt(queries, own_keys)
-        top = jnp.max(scores, axis=1, keepdims=True)
-        weights = jnp.exp2((scores - top) * EXP_SCALE)
-        inverse = 1.0 / jnp.sum(weights, axis=1, keepdims=True)
-        weights = weights.astype(BF16)
+        top = jnp.max(scores[head], axis=1, keepdims=True)
+        weights = jnp.exp2((scores[head] - top) * EXP_SCALE).astype(BF16)
         weights_ref[head] = weights
-        mixed.append(dot_nn(weights, values) * inverse)
+        product = dot_nn(weights, values)
+        inverse = 1.0 / product[:, PAIR:]
+        mixed.append(product[:, :PAIR] * inverse)
         inverses.append(inverse)
     exact = jnp.where(low_half, mixed[0], mixed[1])
     out_ref[...] = exact.astype(BF16)
@@ -163,7 +163,7 @@
     ((2, 1, 1), ((0, 1, 2, 3), (1, 0, 2, 3), (3, 1, 0, 2))),
 )
 FEED_STEPS = ((2, 0), (5, 0), (0, 0), (1, 0), (5, 1), (4, 0), (3, 0), (1, 1), (2, 1), (6, 0), (3, 1), (4, 1), (5, 2), (2, 2), (1, 2), (0, 1), (0, 2), (1, 3), (5, 3), (6, 1), (3, 2), (4, 2), (6, 2), (3, 3), (1, 4), (6, 3), (0, 3), (6, 4), (4, 3), (2, 3), (2, 4), (3, 4), (1, 5), (4, 4), (6, 5), (0, 4), (5, 4), (2, 5), (0, 5), (3, 5), (4, 5), (5, 5), (3, 6), (6, 6), (1, 6), (4, 6), (5, 6), (0, 6), (2, 6))
-FEED_SLOTS = (0, 0, 0, 0, 3, 3, 4, 6, 6, 6, 8, 9, 9, 9, 9, 10, 11, 13, 14, 14, 14, 15, 16, 17, 17, 19, 19, 21, 21, 21, 22, 22, 23, 25, 25, 25, 25, 25, 27, 28, 29, 30, 31, 31, 31, 34, 34, 35, 35)
+FEED_SLOTS = (0, 0, 0, 0, 3, 3, 3, 5, 5, 5, 7, 7, 7, 7, 7, 8, 9, 10, 11, 11, 11, 11, 13, 13, 13, 15, 15, 16, 17, 17, 18, 18, 18, 20, 20, 20, 20, 20, 21, 22, 23, 24, 24, 24, 24, 27, 27, 27, 27)
 REST_PARTS = (
     ((2, 2, 4, 2, 2), ((1, 0, 3, 2), (2, 3, 1, 0), (0, 1, 2, 3), (1, 0, 3, 2), (2, 1, 0, 3))),
     ((1, 1), ((0, 2, 1, 3), (1, 0, 3, 2))),

time: 511 us -> 492 us (0.963)
  Pallas kernels: 270 us -> 254 us
    pallas_call x1, Pallas kernels: 49.2 us -> 38.6 us  [attend(): pl.pallas_call(attend_kernel, grid=(pairs, rows // block), in_specs=[tile...]
    pallas_call x1, Pallas kernels: 113 us -> 105 us  [attend_back(): pl.pallas_call(functools.partial(attend_back_kernel, parts, plan, slots,...]
  transfers between devices with their start and end apart: 37 -> 37, of which waited for: 8 -> 8; matrix products, arithmetic and copies ran while one was open for 10% -> 10% of each run, Pallas kernels for 17% -> 18%
where the time goes in v1:
time: 492 us; the launch traced here: 482 us
  Pallas kernels  254 us (52%)
  waiting for transfers between devices  67.4 us (14%)
  matrix products  63.2 us (13%)
  other arithmetic  39.1 us (8%)
  starting transfers between devices  31.3 us (6%)
  local copies, waits for them, and re-layouts  25.4 us (5%)
    pallas_call x1, Pallas kernels, attend_back(): pl.pallas_call(functools.partial(attend_back_kernel, parts, plan, slots,...  105 us
    pallas_call x1, Pallas kernels, rest_sums(): pl.pallas_call(functools.partial(rest_kernel, parts, plan, bits, len(sour...  76.2 us
    ppermute x28, waiting for transfers between devices, swap_bit(): return lax.ppermute(values, 'dp', [(j, j ^ 1 << bit) for j in range(n)])  60.9 us
    pallas_call x1, Pallas kernels, attend(): pl.pallas_call(attend_kernel, grid=(pairs, rows // block), in_specs=[tile...  38.6 us
    ppermute x28, starting transfers between devices, swap_bit(): return lax.ppermute(values, 'dp', [(j, j ^ 1 << bit) for j in range(n)])  29.7 us
    dot_general x7, matrix products, dot_nn(): lax.dot_general(a, b, (((1,), (0,)), ((), ())), preferred_element_type=F32)  25.1 us
    dot_general x2, matrix products, dot_tn(): lax.dot_general(a, b, (((0,), (0,)), ((), ())), preferred_element_type=F32)  22 us
    pallas_call x1, Pallas kernels, feed(): pl.pallas_call(functools.partial(feed_kernel, chunk=chunk), grid=(rows //...  21.2 us
  transfers between devices with their start and end apart: 37, of which 8 were waited for; matrix products, arithmetic and copies ran while one was open for 10% of the time, Pallas kernels for 18%

profile of v1, /device:TPU:0, one launch (start us, length us, event | category | flops | bytes accessed | tf_op | source)
XLA Modules:
  0.0 482.5 jit_solution(2694497380882145992)
XLA Ops:
  0.7 1.7 constant_dynamic-slice_fusion.16
  4.9 2.6 fusion.5.refs_9_
  7.5 3.0 convolution_convert_fusion.2.k_ref.refs_1_
  10.5 3.0 add_convert_fusion.4.v_ref.refs_2_
  13.6 3.0 add_convert_fusion.5.q_ref.refs_0_
  16.6 38.6 %attend.1 = (bf16[1568,512]{1,0:T(8,128)(2,1)}, f32[1568,512]{1,0:T(8,128)}, f32[1568,512]{1,0:T(8,128)}, bf16[8,1568,1568]{2,1,0:T(8,128)(2,1)}) custom-call(bf16[1568,512]{1,0:T(8,128)(2,1)} %add_convert_fusion.5.q_ref.refs_0_, bf16[1568,512]{1,0:T(8,128)(2,1)} %convolution_convert_fusion.2.k_ref.refs_1_, bf16[1568,512]{1,0:T(8,128)(2,1)} %add_convert_fusion.4.v_ref.refs_2_), custom_call_target="tpu_custom_call" | custom-call | flops 20141047808 | bytes 39337984 | tf_op jit(solution)/shard_map/attend/pallas_call | solution.py:65
  55.3 2.3 convolution_convert_fusion.3
  58.1 3.1 collective-permute-done
  61.2 1.3 fusion.53
  63.3 1.7 add_convert_fusion.3
  65.5 2.2 constant_dynamic-slice_fusion.14
  67.7 2.1 pad_maximum_fusion.2.c_ref
  69.8 3.9 pad_maximum_fusion.1.n_ref
  73.7 21.2 %feed.1 = (bf16[1568,2048]{1,0:T(8,128)(2,1)}, bf16[1568,2048]{1,0:T(8,128)(2,1)}, f32[1,2048]{1,0:T(1,128)}) custom-call(bf16[1568,1024]{1,0:T(8,128)(2,1)} %pad_maximum_fusion.1.n_ref, bf16[1568,1024]{1,0:T(8,128)(2,1)} %pad_maximum_fusion.2.c_ref, bf16[1024,2048]{1,0:T(8,128)(2,1)} %expand_ref.1, bf16[2048,1024]{1,0:T(8,128)(2,1)} %reduce_ref.1, ...), custom_call_target="tpu_custom_call" | custom-call | flops 13153337344 | bytes 38535168 | tf_op jit(solution)/shard_map/feed/pallas_call | solution.py:113
  94.9 10.6 %convolution_convert_fusion.1.refs_10_ = bf16[2048,1024]{1,0:T(8,128)(2,1)S(1)} fusion(bf16[1568,2048]{1,0:T(8,128)(2,1)} %get-tuple-element.113, bf16[784,1024]{1,0:T(8,128)(2,1)} %copy-done.5, bf16[784,1024]{1,0:T(8,128)(2,1)S(1)} %get-tuple-element.182), kind=kOutput, calls=%fused_computation.20 | convolution fusion | flops 6585188352 | bytes 13828096 | tf_op jit(solution)/shard_map/dot_general | solution.py:36
  105.6 11.4 %convolution_convert_fusion.refs_11_ = bf16[1024,2048]{1,0:T(8,128)(2,1)S(1)} fusion(bf16[1568,2048]{1,0:T(8,128)(2,1)S(1)} %copy-done.56, bf16[784,1024]{1,0:T(8,128)(2,1)} %collective-permute-done.1, bf16[784,1024]{1,0:T(8,128)(2,1)} %add_convert_fusion.3), kind=kOutput, calls=%fused_computation.19 | convolution fusion | flops 6585188352 | bytes 13828096 | tf_op jit(solution)/shard_map/dot_general | solution.py:36
  117.0 1.1 constant_dynamic-slice_fusion.9
  119.2 1.3 constant_dynamic-slice_fusion.10
  120.6 1.5 copy-done.42
  122.1 3.5 fusion.26
  125.8 3.3 collective-permute-done.2
  129.1 4.3 multiply_reduce_fusion
  134.5 2.0 fusion.23
  136.9 2.9 collective-permute-start.4
  139.7 1.6 collective-permute-start.5
  141.3 1.5 collective-permute-start.8
  142.8 2.1 convert_reduce_fusion.2
  145.5 6.8 %collective-permute-done.4.refs_12_ = bf16[256,1024]{1,0:T(8,128)(2,1)} collective-permute-done((bf16[256,1024]{1,0:T(8,128)(2,1)}, bf16[256,1024]{1,0:T(8,128)(2,1)}, u32[]{:S(2)}, u32[]{:S(2)}) %collective-permute-start.4) | collective-permute-done | bytes 524320 | tf_op jit(solution)/shard_map/ppermute | solution.py:196
  152.3 1.7 collective-permute-start.7
  154.3 2.8 collective-permute-start.10
  157.1 3.9 pad_maximum_fusion.3.refs_6_
  161.1 16.3 %collective-permute-done.6.refs_14_ = bf16[256,1024]{1,0:T(8,128)(2,1)S(1)} collective-permute-done((bf16[256,1024]{1,0:T(8,128)(2,1)S(1)}, bf16[256,1024]{1,0:T(8,128)(2,1)S(1)}, u32[]{:S(2)}, u32[]{:S(2)}) %collective-permute-start.6) | collective-permute-done | bytes 524320 | tf_op jit(solution)/shard_map/ppermute | solution.py:196
  177.4 1.9 collective-permute-done.10.refs_18_
  180.1 105.5 %attend_back.1 = (bf16[1568,512]{1,0:T(8,128)(2,1)}, bf16[1568,512]{1,0:T(8,128)(2,1)}, bf16[1568,512]{1,0:T(8,128)(2,1)}, bf16[512,1024]{1,0:T(8,128)(2,1)}, bf...) custom-call(bf16[1568,512]{1,0:T(8,128)(2,1)} %add_convert_fusion.5., ...), custom_call_target="tpu_custom_call" | custom-call | flops 40282095616 | bytes 39337984 | tf_op jit(solution)/shard_map/attend_back/pallas_call | solution.py:455
  285.6 1.2 constant_dynamic-slice_fusion.4
  286.8 1.1 constant_dynamic-slice_fusion
  287.9 1.3 constant_dynamic-slice_fusion.2
  289.2 1.1 collective-permute-start.16
  291.3 2.2 fusion.35
  297.1 5.4 %fusion.29 = bf16[784,1024]{1,0:T(8,128)(2,1)S(1)} fusion(bf16[2048,1024]{1,0:T(8,128)(2,1)S(1)} %copy-done.43, bf16[1568,2048]{1,0:T(8,128)(2,1)} %get-tuple-element.113), kind=kOutput, calls=%fused_computation.58 | convolution fusion | flops 3289137152 | bytes 9011200 | tf_op jit(solution)/shard_map/dot_general | solution.py:28
  306.0 2.4 convert_reduce_fusion.1
  308.5 2.1 collective-permute-start.20
  310.5 2.0 fusion.10
  312.5 1.6 copy-done
  314.2 1.7 fusion.13
  316.0 7.0 %add_convert_fusion.2 = bf16[784,1024]{1,0:T(8,128)(2,1)} fusion(f32[784,1024]{1,0:T(8,128)S(1)} %copy-done.3, bf16[784,1024]{1,0:T(8,128)(2,1)S(1)} %collective-permute-done.11, f32[1024]{0:T(1024)S(1)} %copy-done.51, bf16[2048,1024]{1,0:T(8,128)(2,1)S(1)} %copy-done.43, bf16[1568,2048]{1,0:T(8,128)(2,1)} %get-tuple-element.113), kind=kOutput, calls=%fused_computation.38 | convolution fusion | flops 3292348416 | bytes 13832192 | tf_op jit(solution)/shard_map/dot_general | solution.py:28
  323.9 1.2 collective-permute-start.21
  327.4 15.5 %collective-permute-done.21.refs_8_ = bf16[128,1024]{1,0:T(8,128)(2,1)S(1)} collective-permute-done((bf16[128,1024]{1,0:T(8,128)(2,1)S(1)}, bf16[128,1024]{1,0:T(8,128)(2,1)S(1)}, u32[]{:S(2)}, u32[]{:S(2)}) %collective-permute-start.21) | collective-permute-done | bytes 262176 | tf_op jit(solution)/shard_map/ppermute | solution.py:196
  344.7 1.1 collective-permute-start.35
  345.8 1.2 collective-permute-start.34
  348.5 76.2 %rest_sums.1 = (bf16[256,512]{1,0:T(8,128)(2,1)}, bf16[256,512]{1,0:T(8,128)(2,1)}, bf16[512,512]{1,0:T(8,128)(2,1)}, bf16[256,512]{1,0:T(8,128)(2,1)}, bf16[256...) custom-call(bf16[3072,512]{1,0:T(8,128)(2,1)} %bitcast.65, ...), custom_call_target="tpu_custom_call" | custom-call | tf_op jit(solution)/shard_map/rest_sums/pallas_call | solution.py:515
  424.8 2.6 collective-permute-start.23
  427.4 4.6 add_convert_fusion
  431.9 14.2 %collective-permute-done.36.refs_13_ = bf16[128,2048]{1,0:T(8,128)(2,1)} collective-permute-done((bf16[128,2048]{1,0:T(8,128)(2,1)}, bf16[128,2048]{1,0:T(8,128)(2,1)}, u32[]{:S(2)}, u32[]{:S(2)}) %collective-permute-start.36) | collective-permute-done | bytes 524320 | tf_op jit(solution)/shard_map/ppermute | solution.py:196
  447.3 1.3 slice_bitcast_fusion.12
  448.6 6.2 %collective-permute-done.26.refs_7_ = bf16[256,512]{1,0:T(8,128)(2,1)S(1)} collective-permute-done((bf16[256,512]{1,0:T(8,128)(2,1)S(1)}, bf16[256,512]{1,0:T(8,128)(2,1)S(1)}, u32[]{:S(2)}, u32[]{:S(2)}) %collective-permute-start.26) | collective-permute-done | bytes 262176 | tf_op jit(solution)/shard_map/ppermute | solution.py:196
  456.8 1.3 slice_bitcast_fusion.19
  458.1 8.2 %join.3 = (f32[2048,1024]{1,0:T(8,128)}, f32[1024,2048]{1,0:T(8,128)}) custom-call(bf16[256,1024]{1,0:T(8,128)(2,1)} %get-tuple-element.150.refs_0_, bf16[256,1024]{1,0:T(8,128)(2,1)} %copy-done.17, bf16[256,1024]{1,0:T(8,128)(2,1)} %get-tuple-element.151.refs_2_, bf16[256,1024]{1,0:T(8,128)(2,1)} %copy-done.18, ...), custom_call_target="tpu_custom_call" | custom-call | flops 4194304 | bytes 25165824 | tf_op jit(solution)/shard_map/join/pallas_call | solution.py:236
  466.4 1.3 slice_bitcast_fusion.13
  469.3 4.5 join.2
  473.8 2.1 broadcast_select_fusion.3
  475.9 2.0 pad_maximum_fusion.4
  477.9 2.1 broadcast_select_fusion.1
  480.1 2.0 pad_maximum_fusion.5
  (196 shorter events, 28.0 us)
Async XLA Ops:
  7.5 6.1 %copy-start.8 = (bf16[1568,1024]{1,0:T(8,128)(2,1)}, bf16[1568,1024]{1,0:T(8,128)(2,1)S(1)}, u32[]{:S(2)}) copy-start(bf16[1568,1024]{1,0:T(8,128)(2,1)S(1)} %fusion.5.refs_9_) | copy-start | bytes 9633796
  16.6 38.6 %copy-start.44 = (bf16[512,1024]{1,0:T(8,128)(2,1)S(1)}, bf16[512,1024]{1,0:T(8,128)(2,1)}, u32[]{:S(2)}) copy-start(bf16[512,1024]{1,0:T(8,128)(2,1)} %refs_7_.1) | copy-start | bytes 3145732
  55.3 6.0 %copy-start.45 = (bf16[512,1024]{1,0:T(8,128)(2,1)S(1)}, bf16[512,1024]{1,0:T(8,128)(2,1)}, u32[]{:S(2)}) copy-start(bf16[512,1024]{1,0:T(8,128)(2,1)} %refs_7_.1) | copy-start | bytes 3145732
  55.3 6.0 %copy-start.50 = (f32[1024]{0:T(1024)S(1)}, f32[1024]{0:T(1024)}, u32[]{:S(2)}) copy-start(f32[1024]{0:T(1024)} %param.22) | copy-start | bytes 12292
  55.3 6.0 %copy-start.55 = (bf16[1568,512]{1,0:T(8,128)(2,1)S(1)}, bf16[1568,512]{1,0:T(8,128)(2,1)}, u32[]{:S(2)}) copy-start(bf16[1568,512]{1,0:T(8,128)(2,1)} %get-tuple-element.87.refs_8_) | copy-start | bytes 4816900
  57.6 3.6 collective-permute-start
  65.1 4.7 collective-permute-start.1
  94.9 10.7 %copy-start.56 = (bf16[1568,2048]{1,0:T(8,128)(2,1)S(1)}, bf16[1568,2048]{1,0:T(8,128)(2,1)}, u32[]{:S(2)}) copy-start(bf16[1568,2048]{1,0:T(8,128)(2,1)} %get-tuple-element.93) | copy-start | bytes 19267588
  105.6 13.6 %copy-start.13 = (bf16[2048,1024]{1,0:T(8,128)(2,1)}, bf16[2048,1024]{1,0:T(8,128)(2,1)S(1)}, u32[]{:S(2)}) copy-start(bf16[2048,1024]{1,0:T(8,128)(2,1)S(1)} %convolution_convert_fusion.1.refs_10_) | copy-start | bytes 12582916
  118.1 3.9 copy-start.42
  122.1 7.0 %copy-start.2 = (f32[784,1024]{1,0:T(8,128)S(1)}, f32[784,1024]{1,0:T(8,128)}, u32[]{:S(2)}) copy-start(f32[784,1024]{1,0:T(8,128)} %copy-done.1) | copy-start | bytes 9633796
  125.6 3.5 collective-permute-start.2
  136.7 17.6 %collective-permute-start.3 = (bf16[784,1024]{1,0:T(8,128)(2,1)}, bf16[784,1024]{1,0:T(8,128)(2,1)}, u32[]{:S(2)}, u32[]{:S(2)}) collective-permute-start(bf16[784,1024]{1,0:T(8,128)(2,1)} %fusion.23), channel_id=1, source_target_pairs={{0,1},{1,0},{2,3},{3,2},{4,5},{5,4},{6,7},{7,6},{8,9},{9,8},{10,11... | collective-permute-start | bytes 4816904 | tf_op jit(solution)/shard_map/ppermute | solution.py:567
  136.9 15.4 %collective-permute-start.4 = (bf16[256,1024]{1,0:T(8,128)(2,1)}, bf16[256,1024]{1,0:T(8,128)(2,1)}, u32[]{:S(2)}, u32[]{:S(2)}) collective-permute-start(bf16[256,1024]{1,0:T(8,128)(2,1)} %get-tuple-element.94), channel_id=1, source_target_pairs={{0,4},{2,6},{4,0},{6,2},{8,12},{10,14},{12,8},{14,10},{16,20},{18,... | collective-permute-start | bytes 1572872 | tf_op jit(solution)/shard_map/ppermute | solution.py:196
  139.7 14.3 %collective-permute-start.5 = (bf16[256,1024]{1,0:T(8,128)(2,1)}, bf16[256,1024]{1,0:T(8,128)(2,1)}, u32[]{:S(2)}, u32[]{:S(2)}) collective-permute-start(bf16[256,1024]{1,0:T(8,128)(2,1)} %get-tuple-element.95), channel_id=1, source_target_pairs={{0,8},{2,10},{4,12},{6,14},{8,0},{10,2},{12,4},{14,6},{16,24},{18,... | collective-permute-start | bytes 1572872 | tf_op jit(solution)/shard_map/ppermute | solution.py:196
  141.3 38.0 %collective-permute-start.8 = (bf16[256,2048]{1,0:T(8,128)(2,1)}, bf16[256,2048]{1,0:T(8,128)(2,1)}, u32[]{:S(2)}, u32[]{:S(2)}) collective-permute-start(bf16[256,2048]{1,0:T(8,128)(2,1)} %constant_dynamic-slice_fusion.9), channel_id=1, source_target_pairs={{0,2},{2,0},{4,6},{6,4},{8,10},{10,8},{12,14},{14,12},{16,18},{18,... | collective-permute-start | bytes 3145736 | tf_op jit(solution)/shard_map/ppermute | solution.py:196
  142.8 9.5 %copy-start.22 = (bf16[256,1024]{1,0:T(8,128)(2,1)S(1)}, bf16[256,1024]{1,0:T(8,128)(2,1)}, u32[]{:S(2)}) copy-start(bf16[256,1024]{1,0:T(8,128)(2,1)} %get-tuple-element.97) | copy-start | bytes 1572868
  142.8 11.2 %copy-start.21 = (bf16[128,2048]{1,0:T(8,128)(2,1)S(1)}, bf16[128,2048]{1,0:T(8,128)(2,1)}, u32[]{:S(2)}) copy-start(bf16[128,2048]{1,0:T(8,128)(2,1)} %get-tuple-element.99) | copy-start | bytes 1572868
  142.8 11.5 %copy-start.20 = (bf16[128,2048]{1,0:T(8,128)(2,1)S(1)}, bf16[128,2048]{1,0:T(8,128)(2,1)}, u32[]{:S(2)}) copy-start(bf16[128,2048]{1,0:T(8,128)(2,1)} %get-tuple-element.100) | copy-start | bytes 1572868
  144.9 32.5 %collective-permute-start.6 = (bf16[256,1024]{1,0:T(8,128)(2,1)S(1)}, bf16[256,1024]{1,0:T(8,128)(2,1)S(1)}, u32[]{:S(2)}, u32[]{:S(2)}) collective-permute-start(bf16[256,1024]{1,0:T(8,128)(2,1)S(1)} %copy-done.23), channel_id=1, source_target_pairs={{0,2},{2,0},{4,6},{6,4},{8,10},{10,8},{12,14},{14,12},{16,18},{18,... | collective-permute-start | bytes 1572872 | tf_op jit(solution)/shard_map/ppermute | solution.py:196
  152.3 25.1 %collective-permute-start.7 = (bf16[256,1024]{1,0:T(8,128)(2,1)S(1)}, bf16[256,1024]{1,0:T(8,128)(2,1)S(1)}, u32[]{:S(2)}, u32[]{:S(2)}) collective-permute-start(bf16[256,1024]{1,0:T(8,128)(2,1)S(1)} %copy-done.22), channel_id=1, source_target_pairs={{0,4},{2,6},{4,0},{6,2},{8,12},{10,14},{12,8},{14,10},{16,20},{18,... | collective-permute-start | bytes 1572872 | tf_op jit(solution)/shard_map/ppermute | solution.py:196
  154.0 23.4 %collective-permute-start.9 = (bf16[128,2048]{1,0:T(8,128)(2,1)S(1)}, bf16[128,2048]{1,0:T(8,128)(2,1)S(1)}, u32[]{:S(2)}, u32[]{:S(2)}) collective-permute-start(bf16[128,2048]{1,0:T(8,128)(2,1)S(1)} %copy-done.21), channel_id=1, source_target_pairs={{0,4},{2,6},{4,0},{6,2},{8,12},{10,14},{12,8},{14,10},{16,20},{18,... | collective-permute-start | bytes 1572872 | tf_op jit(solution)/shard_map/ppermute | solution.py:196
  154.3 25.0 %collective-permute-start.10 = (bf16[128,2048]{1,0:T(8,128)(2,1)S(1)}, bf16[128,2048]{1,0:T(8,128)(2,1)S(1)}, u32[]{:S(2)}, u32[]{:S(2)}) collective-permute-start(bf16[128,2048]{1,0:T(8,128)(2,1)S(1)} %copy-done.20), channel_id=1, source_target_pairs={{0,16},{2,18},{4,20},{6,22},{8,24},{10,26},{12,28},{14,30},{16,0},... | collective-permute-start | bytes 1572872 | tf_op jit(solution)/shard_map/ppermute | solution.py:196
  285.6 5.7 %copy-start.11 = (bf16[1024,3,512]{2,0,1:T(8,128)(2,1)S(1)}, bf16[1024,3,512]{2,0,1:T(8,128)(2,1)}, u32[]{:S(2)}) copy-start(bf16[1024,3,512]{2,0,1:T(8,128)(2,1)} %param.18) | copy-start | bytes 9437188
  289.2 4.3 copy-start.9
  289.2 34.7 %collective-permute-start.16 = (bf16[256,512]{1,0:T(8,128)(2,1)S(1)}, bf16[256,512]{1,0:T(8,128)(2,1)S(1)}, u32[]{:S(2)}, u32[]{:S(2)}) collective-permute-start(bf16[256,512]{1,0:T(8,128)(2,1)S(1)} %get-tuple-element.125), channel_id=1, source_target_pairs={{0,4},{2,6},{4,0},{6,2},{8,12},{10,14},{12,8},{14,10},{16,20},{18,... | collective-permute-start | bytes 786440 | tf_op jit(solution)/shard_map/ppermute | solution.py:196
  290.3 34.9 %collective-permute-start.17 = (bf16[256,512]{1,0:T(8,128)(2,1)S(1)}, bf16[256,512]{1,0:T(8,128)(2,1)S(1)}, u32[]{:S(2)}, u32[]{:S(2)}) collective-permute-start(bf16[256,512]{1,0:T(8,128)(2,1)S(1)} %get-tuple-element.126), channel_id=1, source_target_pairs={{0,8},{2,10},{4,12},{6,14},{8,0},{10,2},{12,4},{14,6},{16,24},{18,... | collective-permute-start | bytes 786440 | tf_op jit(solution)/shard_map/ppermute | solution.py:196
  290.3 35.9 %collective-permute-start.19 = (bf16[256,512]{1,0:T(8,128)(2,1)S(1)}, bf16[256,512]{1,0:T(8,128)(2,1)S(1)}, u32[]{:S(2)}, u32[]{:S(2)}) collective-permute-start(bf16[256,512]{1,0:T(8,128)(2,1)S(1)} %get-tuple-element.128), channel_id=1, source_target_pairs={{0,4},{2,6},{4,0},{6,2},{8,12},{10,14},{12,8},{14,10},{16,20},{18,... | collective-permute-start | bytes 786440 | tf_op jit(solution)/shard_map/ppermute | solution.py:196
  295.9 12.5 %collective-permute-start.13 = (bf16[784,1024]{1,0:T(8,128)(2,1)S(1)}, bf16[784,1024]{1,0:T(8,128)(2,1)S(1)}, u32[]{:S(2)}, u32[]{:S(2)}) collective-permute-start(bf16[784,1024]{1,0:T(8,128)(2,1)S(1)} %add_convert_fusion.1), channel_id=1, source_target_pairs={{0,1},{1,0},{2,3},{3,2},{4,5},{5,4},{6,7},{7,6},{8,9},{9,8},{10,11... | collective-permute-start | bytes 4816904 | tf_op jit(solution)/shard_map/ppermute | solution.py:567
  302.5 13.4 %collective-permute-start.11 = (bf16[784,1024]{1,0:T(8,128)(2,1)S(1)}, bf16[784,1024]{1,0:T(8,128)(2,1)S(1)}, u32[]{:S(2)}, u32[]{:S(2)}) collective-permute-start(bf16[784,1024]{1,0:T(8,128)(2,1)S(1)} %fusion.29), channel_id=1, source_target_pairs={{0,1},{1,0},{2,3},{3,2},{4,5},{5,4},{6,7},{7,6},{8,9},{9,8},{10,11... | collective-permute-start | bytes 4816904 | tf_op jit(solution)/shard_map/ppermute | solution.py:567
  306.0 4.5 copy-start.37
  308.5 18.8 %collective-permute-start.20 = (bf16[256,512]{1,0:T(8,128)(2,1)S(1)}, bf16[256,512]{1,0:T(8,128)(2,1)S(1)}, u32[]{:S(2)}, u32[]{:S(2)}) collective-permute-start(bf16[256,512]{1,0:T(8,128)(2,1)S(1)} %get-tuple-element.129), channel_id=1, source_target_pairs={{0,8},{2,10},{4,12},{6,14},{8,0},{10,2},{12,4},{14,6},{16,24},{18,... | collective-permute-start | bytes 786440 | tf_op jit(solution)/shard_map/ppermute | solution.py:196
  315.9 10.3 %copy-start.14 = (bf16[256,1024]{1,0:T(8,128)(2,1)S(1)}, bf16[256,1024]{1,0:T(8,128)(2,1)}, u32[]{:S(2)}) copy-start(bf16[256,1024]{1,0:T(8,128)(2,1)} %get-tuple-element.150.refs_0_) | copy-start | bytes 1572868
  315.9 11.4 %copy-start.15 = (bf16[256,1024]{1,0:T(8,128)(2,1)S(1)}, bf16[256,1024]{1,0:T(8,128)(2,1)}, u32[]{:S(2)}) copy-start(bf16[256,1024]{1,0:T(8,128)(2,1)} %get-tuple-element.151.refs_2_) | copy-start | bytes 1572868
  315.9 27.0 %copy-start.16 = (bf16[256,1024]{1,0:T(8,128)(2,1)S(1)}, bf16[256,1024]{1,0:T(8,128)(2,1)}, u32[]{:S(2)}) copy-start(bf16[256,1024]{1,0:T(8,128)(2,1)} %get-tuple-element.152.refs_4_) | copy-start | bytes 1572868
  315.9 31.1 %copy-start.39 = (f32[1,2048]{1,0:T(1,128)S(1)}, f32[1,2048]{1,0:T(1,128)}, u32[]{:S(2)}) copy-start(f32[1,2048]{1,0:T(1,128)} %get-tuple-element.124) | copy-start | bytes 24580
  315.9 7.1 %collective-permute-start.15 = (f32[4,1024]{1,0:T(4,128)S(1)}, f32[4,1024]{1,0:T(4,128)S(1)}, u32[]{:S(2)}, u32[]{:S(2)}) collective-permute-start(f32[4,1024]{1,0:T(4,128)S(1)} %pad_maximum_fusion.6), channel_id=1, source_target_pairs={{0,1},{1,0},{2,3},{3,2},{4,5},{5,4},{6,7},{7,6},{8,9},{9,8},{10,11... | collective-permute-start | bytes 49160 | tf_op jit(solution)/shard_map/ppermute | solution.py:567
  323.0 21.7 %collective-permute-start.18 = (bf16[512,512]{1,0:T(8,128)(2,1)S(1)}, bf16[512,512]{1,0:T(8,128)(2,1)S(1)}, u32[]{:S(2)}, u32[]{:S(2)}) collective-permute-start(bf16[512,512]{1,0:T(8,128)(2,1)S(1)} %constant_dynamic-slice_fusion.4), channel_id=1, source_target_pairs={{0,2},{2,0},{4,6},{6,4},{8,10},{10,8},{12,14},{14,12},{16,18},{18,... | collective-permute-start | bytes 1572872 | tf_op jit(solution)/shard_map/ppermute | solution.py:196
  323.9 24.5 %copy-start.25 = (bf16[256,512]{1,0:T(8,128)(2,1)}, bf16[256,512]{1,0:T(8,128)(2,1)S(1)}, u32[]{:S(2)}) copy-start(bf16[256,512]{1,0:T(8,128)(2,1)S(1)} %collective-permute-done.16.refs_3_) | copy-start | bytes 786436
  323.9 18.9 %collective-permute-start.21 = (bf16[128,1024]{1,0:T(8,128)(2,1)S(1)}, bf16[128,1024]{1,0:T(8,128)(2,1)S(1)}, u32[]{:S(2)}, u32[]{:S(2)}) collective-permute-start(bf16[128,1024]{1,0:T(8,128)(2,1)S(1)} %get-tuple-element.130), channel_id=1, source_target_pairs={{0,2},{2,0},{4,6},{6,4},{8,10},{10,8},{12,14},{14,12},{16,18},{18,... | collective-permute-start | bytes 786440 | tf_op jit(solution)/shard_map/ppermute | solution.py:196
  325.2 22.0 %copy-start.26 = (bf16[256,512]{1,0:T(8,128)(2,1)}, bf16[256,512]{1,0:T(8,128)(2,1)S(1)}, u32[]{:S(2)}) copy-start(bf16[256,512]{1,0:T(8,128)(2,1)S(1)} %collective-permute-done.17.refs_4_) | copy-start | bytes 786436
  325.2 18.6 %collective-permute-start.22 = (bf16[128,1024]{1,0:T(8,128)(2,1)S(1)}, bf16[128,1024]{1,0:T(8,128)(2,1)S(1)}, u32[]{:S(2)}, u32[]{:S(2)}) collective-permute-start(bf16[128,1024]{1,0:T(8,128)(2,1)S(1)} %get-tuple-element.131), channel_id=1, source_target_pairs={{0,4},{2,6},{4,0},{6,2},{8,12},{10,14},{12,8},{14,10},{16,20},{18,... | collective-permute-start | bytes 786440 | tf_op jit(solution)/shard_map/ppermute | solution.py:196
  326.2 20.9 %copy-start.27 = (bf16[256,512]{1,0:T(8,128)(2,1)}, bf16[256,512]{1,0:T(8,128)(2,1)S(1)}, u32[]{:S(2)}) copy-start(bf16[256,512]{1,0:T(8,128)(2,1)S(1)} %collective-permute-done.19.refs_6_) | copy-start | bytes 786436
  326.2 19.6 %collective-permute-start.30 = (bf16[256,1024]{1,0:T(8,128)(2,1)S(1)}, bf16[256,1024]{1,0:T(8,128)(2,1)S(1)}, u32[]{:S(2)}, u32[]{:S(2)}) collective-permute-start(bf16[256,1024]{1,0:T(8,128)(2,1)S(1)} %copy-done.14), channel_id=1, source_target_pairs={{0,4},{2,6},{4,0},{6,2},{8,12},{10,14},{12,8},{14,10},{16,20},{18,... | collective-permute-start | bytes 1572872 | tf_op jit(solution)/shard_map/ppermute | solution.py:196
  327.3 19.9 %copy-start.28 = (bf16[256,512]{1,0:T(8,128)(2,1)}, bf16[256,512]{1,0:T(8,128)(2,1)S(1)}, u32[]{:S(2)}) copy-start(bf16[256,512]{1,0:T(8,128)(2,1)S(1)} %collective-permute-done.20.refs_7_) | copy-start | bytes 786436
  327.3 19.8 %collective-permute-start.31 = (bf16[256,1024]{1,0:T(8,128)(2,1)S(1)}, bf16[256,1024]{1,0:T(8,128)(2,1)S(1)}, u32[]{:S(2)}, u32[]{:S(2)}) collective-permute-start(bf16[256,1024]{1,0:T(8,128)(2,1)S(1)} %copy-done.15), channel_id=1, source_target_pairs={{0,8},{2,10},{4,12},{6,14},{8,0},{10,2},{12,4},{14,6},{16,24},{18,... | collective-permute-start | bytes 1572872 | tf_op jit(solution)/shard_map/ppermute | solution.py:196
  342.9 4.3 copy-start.30
  342.9 81.8 %collective-permute-start.32 = (bf16[256,1024]{1,0:T(8,128)(2,1)S(1)}, bf16[256,1024]{1,0:T(8,128)(2,1)}, u32[]{:S(2)}, u32[]{:S(2)}) collective-permute-start(bf16[256,1024]{1,0:T(8,128)(2,1)S(1)} %copy-done.16), channel_id=1, source_target_pairs={{0,2},{2,0},{4,6},{6,4},{8,10},{10,8},{12,14},{14,12},{16,18},{18,... | collective-permute-start | bytes 1572872 | tf_op jit(solution)/shard_map/ppermute | solution.py:196
  343.7 81.0 %collective-permute-start.33 = (bf16[256,1024]{1,0:T(8,128)(2,1)}, bf16[256,1024]{1,0:T(8,128)(2,1)}, u32[]{:S(2)}, u32[]{:S(2)}) collective-permute-start(bf16[256,1024]{1,0:T(8,128)(2,1)} %get-tuple-element.153.refs_6_), channel_id=1, source_target_pairs={{0,4},{2,6},{4,0},{6,2},{8,12},{10,14},{12,8},{14,10},{16,20},{18,... | collective-permute-start | bytes 1572872 | tf_op jit(solution)/shard_map/ppermute | solution.py:196
  344.7 82.7 %collective-permute-start.35 = (bf16[128,2048]{1,0:T(8,128)(2,1)}, bf16[128,2048]{1,0:T(8,128)(2,1)}, u32[]{:S(2)}, u32[]{:S(2)}) collective-permute-start(bf16[128,2048]{1,0:T(8,128)(2,1)} %get-tuple-element.155.refs_10_), channel_id=1, source_target_pairs={{0,4},{2,6},{4,0},{6,2},{8,12},{10,14},{12,8},{14,10},{16,20},{18,... | collective-permute-start | bytes 1572872 | tf_op jit(solution)/shard_map/ppermute | solution.py:196
  345.8 100.3 %collective-permute-start.34 = (bf16[256,2048]{1,0:T(8,128)(2,1)}, bf16[256,2048]{1,0:T(8,128)(2,1)}, u32[]{:S(2)}, u32[]{:S(2)}) collective-permute-start(bf16[256,2048]{1,0:T(8,128)(2,1)} %get-tuple-element.154.refs_8_), channel_id=1, source_target_pairs={{0,2},{2,0},{4,6},{6,4},{8,10},{10,8},{12,14},{14,12},{16,18},{18,... | collective-permute-start | bytes 3145736 | tf_op jit(solution)/shard_map/ppermute | solution.py:196
  347.1 126.7 %collective-permute-start.12 = (bf16[784,1024]{1,0:T(8,128)(2,1)}, bf16[784,1024]{1,0:T(8,128)(2,1)}, u32[]{:S(2)}, u32[]{:S(2)}) collective-permute-start(bf16[784,1024]{1,0:T(8,128)(2,1)} %add_convert_fusion.2), channel_id=1, source_target_pairs={{0,1},{1,0},{2,3},{3,2},{4,5},{5,4},{6,7},{7,6},{8,9},{9,8},{10,11... | collective-permute-start | bytes 4816904 | tf_op jit(solution)/shard_map/ppermute | solution.py:567
  424.7 21.4 %collective-permute-start.36 = (bf16[128,2048]{1,0:T(8,128)(2,1)}, bf16[128,2048]{1,0:T(8,128)(2,1)}, u32[]{:S(2)}, u32[]{:S(2)}) collective-permute-start(bf16[128,2048]{1,0:T(8,128)(2,1)} %get-tuple-element.156.refs_12_), channel_id=1, source_target_pairs={{0,16},{2,18},{4,20},{6,22},{8,24},{10,26},{12,28},{14,30},{16,0},... | collective-permute-start | bytes 1572872 | tf_op jit(solution)/shard_map/ppermute | solution.py:196
  424.8 21.6 %collective-permute-start.23 = (bf16[256,512]{1,0:T(8,128)(2,1)}, bf16[256,512]{1,0:T(8,128)(2,1)}, u32[]{:S(2)}, u32[]{:S(2)}) collective-permute-start(bf16[256,512]{1,0:T(8,128)(2,1)} %get-tuple-element.141.refs_0_), channel_id=1, source_target_pairs={{0,4},{2,6},{4,0},{6,2},{8,12},{10,14},{12,8},{14,10},{16,20},{18,... | collective-permute-start | bytes 786440 | tf_op jit(solution)/shard_map/ppermute | solution.py:196
  427.4 18.8 %copy-start.29 = (bf16[256,512]{1,0:T(8,128)(2,1)S(1)}, bf16[256,512]{1,0:T(8,128)(2,1)}, u32[]{:S(2)}) copy-start(bf16[256,512]{1,0:T(8,128)(2,1)} %get-tuple-element.144.refs_6_) | copy-start | bytes 786436
  427.4 19.1 %collective-permute-start.24 = (bf16[256,512]{1,0:T(8,128)(2,1)}, bf16[256,512]{1,0:T(8,128)(2,1)}, u32[]{:S(2)}, u32[]{:S(2)}) collective-permute-start(bf16[256,512]{1,0:T(8,128)(2,1)} %get-tuple-element.142.refs_2_), channel_id=1, source_target_pairs={{0,8},{2,10},{4,12},{6,14},{8,0},{10,2},{12,4},{14,6},{16,24},{18,... | collective-permute-start | bytes 786440 | tf_op jit(solution)/shard_map/ppermute | solution.py:196
  446.1 31.8 %collective-permute-start.14 = (bf16[784,1024]{1,0:T(8,128)(2,1)}, bf16[784,1024]{1,0:T(8,128)(2,1)}, u32[]{:S(2)}, u32[]{:S(2)}) collective-permute-start(bf16[784,1024]{1,0:T(8,128)(2,1)} %add_convert_fusion), channel_id=1, source_target_pairs={{0,1},{1,0},{2,3},{3,2},{4,5},{5,4},{6,7},{7,6},{8,9},{9,8},{10,11... | collective-permute-start | bytes 4816904 | tf_op jit(solution)/shard_map/ppermute | solution.py:567
  446.1 8.7 %collective-permute-start.26 = (bf16[256,512]{1,0:T(8,128)(2,1)S(1)}, bf16[256,512]{1,0:T(8,128)(2,1)S(1)}, u32[]{:S(2)}, u32[]{:S(2)}) collective-permute-start(bf16[256,512]{1,0:T(8,128)(2,1)S(1)} %copy-done.29), channel_id=1, source_target_pairs={{0,4},{2,6},{4,0},{6,2},{8,12},{10,14},{12,8},{14,10},{16,20},{18,... | collective-permute-start | bytes 786440 | tf_op jit(solution)/shard_map/ppermute | solution.py:196
  446.4 9.4 %collective-permute-start.27 = (bf16[256,512]{1,0:T(8,128)(2,1)}, bf16[256,512]{1,0:T(8,128)(2,1)S(1)}, u32[]{:S(2)}, u32[]{:S(2)}) collective-permute-start(bf16[256,512]{1,0:T(8,128)(2,1)} %get-tuple-element.145.refs_8_), channel_id=1, source_target_pairs={{0,8},{2,10},{4,12},{6,14},{8,0},{10,2},{12,4},{14,6},{16,24},{18,... | collective-permute-start | bytes 786440 | tf_op jit(solution)/shard_map/ppermute | solution.py:196
  446.4 21.3 %collective-permute-start.25 = (bf16[512,512]{1,0:T(8,128)(2,1)}, bf16[512,512]{1,0:T(8,128)(2,1)S(1)}, u32[]{:S(2)}, u32[]{:S(2)}) collective-permute-start(bf16[512,512]{1,0:T(8,128)(2,1)} %get-tuple-element.143.refs_4_), channel_id=1, source_target_pairs={{0,2},{2,0},{4,6},{6,4},{8,10},{10,8},{12,14},{14,12},{16,18},{18,... | collective-permute-start | bytes 1572872 | tf_op jit(solution)/shard_map/ppermute | solution.py:196
  454.8 11.5 %copy-start.32 = (bf16[256,512]{1,0:T(8,128)(2,1)}, bf16[256,512]{1,0:T(8,128)(2,1)S(1)}, u32[]{:S(2)}) copy-start(bf16[256,512]{1,0:T(8,128)(2,1)S(1)} %collective-permute-done.26.refs_7_) | copy-start | bytes 786436
  454.8 12.8 %collective-permute-start.28 = (bf16[128,1024]{1,0:T(8,128)(2,1)}, bf16[128,1024]{1,0:T(8,128)(2,1)S(1)}, u32[]{:S(2)}, u32[]{:S(2)}) collective-permute-start(bf16[128,1024]{1,0:T(8,128)(2,1)} %get-tuple-element.146.refs_10_), channel_id=1, source_target_pairs={{0,2},{2,0},{4,6},{6,4},{8,10},{10,8},{12,14},{14,12},{16,18},{18,... | collective-permute-start | bytes 786440 | tf_op jit(solution)/shard_map/ppermute | solution.py:196
  455.8 10.6 %copy-start.33 = (bf16[256,512]{1,0:T(8,128)(2,1)}, bf16[256,512]{1,0:T(8,128)(2,1)S(1)}, u32[]{:S(2)}) copy-start(bf16[256,512]{1,0:T(8,128)(2,1)S(1)} %collective-permute-done.27.refs_9_) | copy-start | bytes 786436
  455.8 11.9 %collective-permute-start.29 = (bf16[128,1024]{1,0:T(8,128)(2,1)}, bf16[128,1024]{1,0:T(8,128)(2,1)S(1)}, u32[]{:S(2)}, u32[]{:S(2)}) collective-permute-start(bf16[128,1024]{1,0:T(8,128)(2,1)} %get-tuple-element.147.refs_12_), channel_id=1, source_target_pairs={{0,4},{2,6},{4,0},{6,2},{8,12},{10,14},{12,8},{14,10},{16,20},{18,... | collective-permute-start | bytes 786440 | tf_op jit(solution)/shard_map/ppermute | solution.py:196
  (30 other events, 59.5 us)
